TPU v7x, 256 devices: a 8x8x2 block of a 8x8x16 slice. The times are simulated.
256 devices in a mesh: grp: 2 (over z), row: 128 (over y, x, core).
Axes of the slice: x: 8, y: 8, z: 2, core: 2. Of those that a mesh axis runs over, the one named last changes fastest.
The devices are a block of a 8x8x16 slice.
Arguments:
- source_emb: bfloat16 [1048576, 256], P(('grp', 'row')), parts along dimension 0, may hold values from -6 to 6
- target_emb: bfloat16 [1048576, 256], P(('grp', 'row')), parts along dimension 0, may hold values from -6 to 6
- source_cluster: int32 [1048576], P(('grp', 'row')), parts along dimension 0, may hold values from 0 to 4095, never falling along the last dimension, each value on 1 to 256 neighbouring positions
- target_cluster: int32 [1048576], P(('grp', 'row')), parts along dimension 0, may hold values from 0 to 4095, never falling along the last dimension, each value on 1 to 256 neighbouring positions
- coarse_source: float32 [8192], P('grp'), parts along dimension 0, may hold values from -3 to 3
- coarse_target: float32 [8192], P('grp'), parts along dimension 0, may hold values from -3 to 3
- block_list: int32 [8192, 8], P(('grp', 'row')), parts along dimension 0, may hold values from 0 to 4095, as said below
- block_count: int32 [8192], P(('grp', 'row')), parts along dimension 0, may hold values from 1 to 8, as said below
Outputs:
- source_potential: float32 [1048576], P(('grp', 'row')), parts along dimension 0
- target_potential: float32 [1048576], P(('grp', 'row')), parts along dimension 0
There are 2 independent parts, one for each index of `grp`. A program takes and returns all parts, laid end to end along the dimension named above; each array names one. Nothing has to cross between parts.
Inputs may be any that keep to these rules, and one draw needn't show every extreme that they name: Each row of block_list names 8 different target tiles, each within 1 device of the source tile's device (tile index divided by 32); entry 0 is the target tile with the source tile's own index. Only the first block_count entries of a row are active. `block_count`: some source tile has 8 active entries in every draw.
All inputs are finite; a program needn't handle non-finite values.
Results may differ from a plain program's by a relative error of at most 0.0003.
Values may be sent and summed in bfloat16 or wider, within the bound.
A program may use at most 64 MiB of HBM per device.

v0:
```python
import jax
import jax.numpy as jnp
from jax import lax
from jax.sharding import PartitionSpec as P

TILE = 128
REACH = 1
ITERS = 2


EPSILON = 0.5
NEGATIVE = -1e30


def shifted_2(block, axis, distance):
    devices = range(lax.axis_size(axis))
    route = [(i - distance, i) for i in devices if i - distance in devices]
    return lax.ppermute(block, axis, route)


def stable_lse(values, reduce_dim):
    highest = jnp.max(values, axis=reduce_dim, keepdims=True)
    return jnp.squeeze(highest, reduce_dim) + jnp.log(
        jnp.sum(jnp.exp(values - highest), axis=reduce_dim)
    )


def coarse_lookup(coarse_table, labels):
    matches = labels[:, None] == jnp.arange(coarse_table.shape[0], dtype=jnp.int32)[None, :]
    return jnp.sum(jnp.where(matches, coarse_table[None, :], 0.0), axis=1)


def target_window(shard_rows):
    pieces = []
    for offset in range(-REACH, REACH + 1):
        if offset == 0:
            pieces.append(shard_rows)
        else:
            pieces.append(shifted_2(shard_rows, "row", -offset))
    return jnp.concatenate(pieces, axis=0)


def duals_window(shard_duals):
    pieces = []
    for offset in range(-REACH, REACH + 1):
        if offset == 0:
            pieces.append(shard_duals)
        else:
            pieces.append(shifted_2(shard_duals, "row", -offset))
    return jnp.concatenate(pieces, axis=0)


def merge_columns(col_part, row_count):
    pieces = col_part.reshape(2 * REACH + 1, row_count)
    my_index = lax.axis_index("row")
    peers = lax.axis_size("row")
    arrived = []
    for offset in range(-REACH, REACH + 1):
        if offset == 0:
            arrived.append(pieces[REACH])
        else:
            shifted = shifted_2(pieces[offset + REACH], "row", offset)
            sender = my_index - offset
            inside = (sender >= 0) & (sender < peers)
            arrived.append(jnp.where(inside, shifted, NEGATIVE))
    stacked = jnp.stack(arrived)
    return stable_lse(stacked, 0)


def listed_pass(
    source_emb,
    window,
    source_pot,
    target_near,
    local_ids,
    live,
    block_count,
    tile_total,
    span_tiles,
):
    width = source_emb.shape[1]
    source_tiles = source_emb.reshape(tile_total, TILE, width)
    window_tiles = window.reshape(span_tiles, TILE, width)
    near_grid = target_near.reshape(span_tiles, TILE)
    source_grid = source_pot.reshape(tile_total, TILE)

    def one_turn(slot_index, carry):
        row_max, row_total, col_max, col_total = carry
        picked = lax.dynamic_index_in_dim(local_ids, slot_index, 1, keepdims=False)
        active_now = lax.dynamic_index_in_dim(live, slot_index, 1, keepdims=False)
        chosen = jnp.take(window_tiles, picked, axis=0)
        scores = jnp.einsum(
            "tre,tce->trc", source_tiles, chosen, preferred_element_type=jnp.float32
        )
        row_terms = (jnp.take(near_grid, picked, axis=0)[:, None, :] + scores) / EPSILON
        row_terms = jnp.where(active_now[:, None, None], row_terms, NEGATIVE)
        row_upper = jnp.maximum(row_max, jnp.max(row_terms, axis=2))
        row_total = row_total * jnp.exp(row_max - row_upper) + jnp.sum(
            jnp.exp(row_terms - row_upper[:, :, None]), axis=2
        )
        col_terms = (source_grid[:, :, None] + scores) / EPSILON
        part_max = jnp.max(col_terms, axis=1)
        part_total = jnp.sum(jnp.exp(col_terms - part_max[:, None, :]), axis=1)
        part_max = jnp.where(active_now[:, None], part_max, NEGATIVE)
        part_total = jnp.where(active_now[:, None], part_total, 0.0)
        col_upper = col_max.at[picked].max(part_max)
        added = (
            jnp.zeros_like(col_total)
            .at[picked]
            .add(part_total * jnp.exp(part_max - jnp.take(col_upper, picked, axis=0)))
        )
        col_total = col_total * jnp.exp(col_max - col_upper) + added
        return (row_upper, row_total, col_upper, col_total)

    starting = (
        jnp.full((tile_total, TILE), NEGATIVE, jnp.float32),
        jnp.zeros((tile_total, TILE), jnp.float32),
        jnp.full((span_tiles, TILE), NEGATIVE, jnp.float32),
        jnp.zeros((span_tiles, TILE), jnp.float32),
    )
    turn_limit = jnp.max(block_count)
    row_max, row_total, col_max, col_total = lax.fori_loop(0, turn_limit, one_turn, starting)
    row_lse = (row_max + jnp.log(row_total)).reshape(tile_total * TILE)
    positive = col_total > 0
    col_part = jnp.where(positive, col_max + jnp.log(jnp.where(positive, col_total, 1.0)), NEGATIVE)
    return (row_lse, col_part.reshape(span_tiles * TILE))


def shards(
    source_emb,
    target_emb,
    source_cluster,
    target_cluster,
    coarse_source,
    coarse_target,
    block_list,
    block_count,
):
    row_count = source_emb.shape[0]
    tile_total = row_count // TILE
    span_tiles = (2 * REACH + 1) * tile_total
    peers = lax.axis_size("row")
    first_tile = (lax.axis_index("row") - REACH) * tile_total
    local_ids = block_list - first_tile
    live = jnp.arange(block_list.shape[1], dtype=jnp.int32)[None, :] < block_count[:, None]
    log_size = EPSILON * jnp.log(jnp.float32(row_count * peers))
    source_pot = coarse_lookup(coarse_source, source_cluster)
    target_pot = coarse_lookup(coarse_target, target_cluster)
    window = target_window(target_emb)
    for iteration in range(ITERS):
        target_near = duals_window(target_pot)
        row_lse, col_part = listed_pass(
            source_emb,
            window,
            source_pot,
            target_near,
            local_ids,
            live,
            block_count,
            tile_total,
            span_tiles,
        )
        col_lse = merge_columns(col_part, row_count)
        source_next = 0.5 * (source_pot + log_size - EPSILON * row_lse)
        target_next = 0.5 * (target_pot + log_size - EPSILON * col_lse)
        source_pot, target_pot = (source_next, target_next)
    return (source_pot, target_pot)


def solution(mesh):
    placed = (
        P(("grp", "row"), None),
        P(("grp", "row"), None),
        P(("grp", "row")),
        P(("grp", "row")),
        P("grp"),
        P("grp"),
        P(("grp", "row"), None),
        P(("grp", "row")),
    )
    return jax.shard_map(
        shards,
        mesh=mesh,
        in_specs=placed,
        out_specs=(P(("grp", "row")), P(("grp", "row"))),
        check_vma=False,
    )
```

profile of v0, /device:TPU:575, one launch (start us, length us, event | category | flops | bytes accessed | tf_op | source)
XLA Modules:
  0.0 331.6 jit_solution(13054125176116860384)
XLA Ops:
  0.6 12.1 %select_reduce_fusion = f32[4096]{0:T(1024)S(1)} fusion(f32[4096]{0:T(1024)} %param.21, s32[4096]{0:T(1024)} %param.19), kind=kLoop, calls=%fused_computation.92 | loop fusion | flops 50327552 | bytes 49152 | tf_op jit(solution)/shard_map/reduce_sum | solution.py:30
  12.7 5.0 %collective-permute-start = (f32[4096]{0:T(1024)S(1)}, f32[4096]{0:T(1024)S(1)}, u32[]{:S(2)}, u32[]{:S(2)}) collective-permute-start(f32[4096]{0:T(1024)S(1)} %select_reduce_fusion), channel_id=1, source_target_pairs={{0,1},{1,2},{2,3},{3,4},{4,5},{5,6},{6,7},{7,8},{8,9},{9,10},{10,1... | collective-permute-start | bytes 49160 | tf_op jit(solution)/shard_map/ppermute | solution.py:18
  17.7 2.0 collective-permute-start.1
  19.7 7.0 %collective-permute-start.2 = (bf16[4096,256]{1,0:T(8,128)(2,1)}, bf16[4096,256]{1,0:T(8,128)(2,1)S(1)}, u32[]{:S(2)}, u32[]{:S(2)}) collective-permute-start(bf16[4096,256]{1,0:T(8,128)(2,1)} %param.17), channel_id=1, source_target_pairs={{0,1},{1,2},{2,3},{3,4},{4,5},{5,6},{6,7},{7,8},{8,9},{9,10},{10,1... | collective-permute-start | bytes 6291464 | tf_op jit(solution)/shard_map/ppermute | solution.py:18
  26.7 2.0 collective-permute-start.3
  29.3 12.0 %select_reduce_fusion.1 = f32[4096]{0:T(1024)S(1)} fusion(f32[4096]{0:T(1024)} %param.20, s32[4096]{0:T(1024)} %param.18), kind=kLoop, calls=%fused_computation.94 | loop fusion | flops 50327552 | bytes 49152 | tf_op jit(solution)/shard_map/reduce_sum | solution.py:30
  43.3 6.7 %collective-permute-done.2 = bf16[4096,256]{1,0:T(8,128)(2,1)S(1)} collective-permute-done((bf16[4096,256]{1,0:T(8,128)(2,1)}, bf16[4096,256]{1,0:T(8,128)(2,1)S(1)}, u32[]{:S(2)}, u32[]{:S(2)}) %collective-permute-start.2) | collective-permute-done | bytes 2097184 | tf_op jit(solution)/shard_map/ppermute | solution.py:18
  50.0 7.8 %collective-permute-done.3 = bf16[4096,256]{1,0:T(8,128)(2,1)} collective-permute-done((bf16[4096,256]{1,0:T(8,128)(2,1)}, bf16[4096,256]{1,0:T(8,128)(2,1)}, u32[]{:S(2)}, u32[]{:S(2)}) %collective-permute-start.3) | collective-permute-done | bytes 2097184 | tf_op jit(solution)/shard_map/ppermute | solution.py:18
  57.7 15.0 %pad_maximum_fusion = bf16[12288,256]{1,0:T(8,128)(2,1)} fusion(bf16[4096,256]{1,0:T(8,128)(2,1)} %collective-permute-done.3, bf16[4096,256]{1,0:T(8,128)(2,1)} %param.17, bf16[4096,256]{1,0:T(8,128)(2,1)S(1)} %collective-permute-done.2), kind=kLoop, calls=%fused_computation.96 | loop fusion | flops 18874368 | bytes 12582912 | tf_op jit(solution)/shard_map/concatenate | solution.py:40
  72.8 111.1 %while.32 = (s32[]{:T(128)}, f32[32,128]{1,0:T(8,128)S(1)}, f32[32,128]{1,0:T(8,128)S(1)}, f32[96,128]{1,0:T(8,128)S(1)}, f32[96,128]{1,0:T(8,128)S(1)}, /*index...) while((s32[]{:T(128)}, f32[32,128]{1,0:T(8,128)S(1)}, ...), condition=%wide.region_10.13_spmd, body=%wide.region_3.12_spmd.sunk | while | flops 277935392 | bytes 13577027 | solution.py:122
  74.1 4.8 %gather_fusion.1 = bf16[32,128,256]{2,1,0:T(8,128)(2,1)} fusion(bf16[96,128,256]{2,1,0:T(8,128)(2,1)} %get-tuple-element.439, s32[1024]{0:T(1024)S(1)} %pad_clamp_fusion.4), kind=kCustom, calls=%fused_computation.1.clone.clone.1 | custom fusion | bytes 4194432 | tf_op jit(solution)/shard_map/while/body/jit(_take)/gather | solution.py:91
  78.9 3.7 %bitcast_reduce_fusion.6 = (f32[32,128]{1,0:T(8,128)S(1)}, f32[32,128]{1,0:T(8,128)S(1)}, f32[32,128,128]{2,1,0:T(8,128)S(1)}) fusion(f32[32,128]{1,0:T(8,128)S(1)} %bitcast.127, f32[32,128]{1,0:T(8,128)S(1)} %broadcast_select_fusion.12, pred[32]{0:T(512)(128)(4,1)S(1)} %dynamic-slice_bitcast_fusion.4, ...), kind=kOutput, calls=%fused_computation.11.clone.1 | convolution fusion | flops 273145856 | bytes 6357056 | tf_op jit(solution)/shard_map/while/body/tre,tce->trc/dot_general | solution.py:92
  83.5 2.2 fusion.84
  87.9 4.8 %gather_fusion.1 = bf16[32,128,256]{2,1,0:T(8,128)(2,1)} fusion(bf16[96,128,256]{2,1,0:T(8,128)(2,1)} %get-tuple-element.439, s32[1024]{0:T(1024)S(1)} %pad_clamp_fusion.4), kind=kCustom, calls=%fused_computation.1.clone.clone.1 | custom fusion | bytes 4194432 | tf_op jit(solution)/shard_map/while/body/jit(_take)/gather | solution.py:91
  92.7 3.7 %bitcast_reduce_fusion.6 = (f32[32,128]{1,0:T(8,128)S(1)}, f32[32,128]{1,0:T(8,128)S(1)}, f32[32,128,128]{2,1,0:T(8,128)S(1)}) fusion(f32[32,128]{1,0:T(8,128)S(1)} %bitcast.127, f32[32,128]{1,0:T(8,128)S(1)} %broadcast_select_fusion.12, pred[32]{0:T(512)(128)(4,1)S(1)} %dynamic-slice_bitcast_fusion.4, ...), kind=kOutput, calls=%fused_computation.11.clone.1 | convolution fusion | flops 273145856 | bytes 6357056 | tf_op jit(solution)/shard_map/while/body/tre,tce->trc/dot_general | solution.py:92
  97.3 2.2 fusion.84
  101.7 4.8 %gather_fusion.1 = bf16[32,128,256]{2,1,0:T(8,128)(2,1)} fusion(bf16[96,128,256]{2,1,0:T(8,128)(2,1)} %get-tuple-element.439, s32[1024]{0:T(1024)S(1)} %pad_clamp_fusion.4), kind=kCustom, calls=%fused_computation.1.clone.clone.1 | custom fusion | bytes 4194432 | tf_op jit(solution)/shard_map/while/body/jit(_take)/gather | solution.py:91
  106.5 3.7 %bitcast_reduce_fusion.6 = (f32[32,128]{1,0:T(8,128)S(1)}, f32[32,128]{1,0:T(8,128)S(1)}, f32[32,128,128]{2,1,0:T(8,128)S(1)}) fusion(f32[32,128]{1,0:T(8,128)S(1)} %bitcast.127, f32[32,128]{1,0:T(8,128)S(1)} %broadcast_select_fusion.12, pred[32]{0:T(512)(128)(4,1)S(1)} %dynamic-slice_bitcast_fusion.4, ...), kind=kOutput, calls=%fused_computation.11.clone.1 | convolution fusion | flops 273145856 | bytes 6357056 | tf_op jit(solution)/shard_map/while/body/tre,tce->trc/dot_general | solution.py:92
  111.1 2.2 fusion.84
  115.5 4.8 %gather_fusion.1 = bf16[32,128,256]{2,1,0:T(8,128)(2,1)} fusion(bf16[96,128,256]{2,1,0:T(8,128)(2,1)} %get-tuple-element.439, s32[1024]{0:T(1024)S(1)} %pad_clamp_fusion.4), kind=kCustom, calls=%fused_computation.1.clone.clone.1 | custom fusion | bytes 4194432 | tf_op jit(solution)/shard_map/while/body/jit(_take)/gather | solution.py:91
  120.3 3.7 %bitcast_reduce_fusion.6 = (f32[32,128]{1,0:T(8,128)S(1)}, f32[32,128]{1,0:T(8,128)S(1)}, f32[32,128,128]{2,1,0:T(8,128)S(1)}) fusion(f32[32,128]{1,0:T(8,128)S(1)} %bitcast.127, f32[32,128]{1,0:T(8,128)S(1)} %broadcast_select_fusion.12, pred[32]{0:T(512)(128)(4,1)S(1)} %dynamic-slice_bitcast_fusion.4, ...), kind=kOutput, calls=%fused_computation.11.clone.1 | convolution fusion | flops 273145856 | bytes 6357056 | tf_op jit(solution)/shard_map/while/body/tre,tce->trc/dot_general | solution.py:92
  124.9 2.2 fusion.84
  129.3 4.8 %gather_fusion.1 = bf16[32,128,256]{2,1,0:T(8,128)(2,1)} fusion(bf16[96,128,256]{2,1,0:T(8,128)(2,1)} %get-tuple-element.439, s32[1024]{0:T(1024)S(1)} %pad_clamp_fusion.4), kind=kCustom, calls=%fused_computation.1.clone.clone.1 | custom fusion | bytes 4194432 | tf_op jit(solution)/shard_map/while/body/jit(_take)/gather | solution.py:91
  134.1 3.7 %bitcast_reduce_fusion.6 = (f32[32,128]{1,0:T(8,128)S(1)}, f32[32,128]{1,0:T(8,128)S(1)}, f32[32,128,128]{2,1,0:T(8,128)S(1)}) fusion(f32[32,128]{1,0:T(8,128)S(1)} %bitcast.127, f32[32,128]{1,0:T(8,128)S(1)} %broadcast_select_fusion.12, pred[32]{0:T(512)(128)(4,1)S(1)} %dynamic-slice_bitcast_fusion.4, ...), kind=kOutput, calls=%fused_computation.11.clone.1 | convolution fusion | flops 273145856 | bytes 6357056 | tf_op jit(solution)/shard_map/while/body/tre,tce->trc/dot_general | solution.py:92
  138.7 2.2 fusion.84
  143.1 4.8 %gather_fusion.1 = bf16[32,128,256]{2,1,0:T(8,128)(2,1)} fusion(bf16[96,128,256]{2,1,0:T(8,128)(2,1)} %get-tuple-element.439, s32[1024]{0:T(1024)S(1)} %pad_clamp_fusion.4), kind=kCustom, calls=%fused_computation.1.clone.clone.1 | custom fusion | bytes 4194432 | tf_op jit(solution)/shard_map/while/body/jit(_take)/gather | solution.py:91
  147.9 3.7 %bitcast_reduce_fusion.6 = (f32[32,128]{1,0:T(8,128)S(1)}, f32[32,128]{1,0:T(8,128)S(1)}, f32[32,128,128]{2,1,0:T(8,128)S(1)}) fusion(f32[32,128]{1,0:T(8,128)S(1)} %bitcast.127, f32[32,128]{1,0:T(8,128)S(1)} %broadcast_select_fusion.12, pred[32]{0:T(512)(128)(4,1)S(1)} %dynamic-slice_bitcast_fusion.4, ...), kind=kOutput, calls=%fused_computation.11.clone.1 | convolution fusion | flops 273145856 | bytes 6357056 | tf_op jit(solution)/shard_map/while/body/tre,tce->trc/dot_general | solution.py:92
  152.5 2.2 fusion.84
  156.9 4.8 %gather_fusion.1 = bf16[32,128,256]{2,1,0:T(8,128)(2,1)} fusion(bf16[96,128,256]{2,1,0:T(8,128)(2,1)} %get-tuple-element.439, s32[1024]{0:T(1024)S(1)} %pad_clamp_fusion.4), kind=kCustom, calls=%fused_computation.1.clone.clone.1 | custom fusion | bytes 4194432 | tf_op jit(solution)/shard_map/while/body/jit(_take)/gather | solution.py:91
  161.7 3.7 %bitcast_reduce_fusion.6 = (f32[32,128]{1,0:T(8,128)S(1)}, f32[32,128]{1,0:T(8,128)S(1)}, f32[32,128,128]{2,1,0:T(8,128)S(1)}) fusion(f32[32,128]{1,0:T(8,128)S(1)} %bitcast.127, f32[32,128]{1,0:T(8,128)S(1)} %broadcast_select_fusion.12, pred[32]{0:T(512)(128)(4,1)S(1)} %dynamic-slice_bitcast_fusion.4, ...), kind=kOutput, calls=%fused_computation.11.clone.1 | convolution fusion | flops 273145856 | bytes 6357056 | tf_op jit(solution)/shard_map/while/body/tre,tce->trc/dot_general | solution.py:92
  166.3 2.2 fusion.84
  170.7 4.8 %gather_fusion.1 = bf16[32,128,256]{2,1,0:T(8,128)(2,1)} fusion(bf16[96,128,256]{2,1,0:T(8,128)(2,1)} %get-tuple-element.439, s32[1024]{0:T(1024)S(1)} %pad_clamp_fusion.4), kind=kCustom, calls=%fused_computation.1.clone.clone.1 | custom fusion | bytes 4194432 | tf_op jit(solution)/shard_map/while/body/jit(_take)/gather | solution.py:91
  175.5 3.7 %bitcast_reduce_fusion.6 = (f32[32,128]{1,0:T(8,128)S(1)}, f32[32,128]{1,0:T(8,128)S(1)}, f32[32,128,128]{2,1,0:T(8,128)S(1)}) fusion(f32[32,128]{1,0:T(8,128)S(1)} %bitcast.127, f32[32,128]{1,0:T(8,128)S(1)} %broadcast_select_fusion.12, pred[32]{0:T(512)(128)(4,1)S(1)} %dynamic-slice_bitcast_fusion.4, ...), kind=kOutput, calls=%fused_computation.11.clone.1 | convolution fusion | flops 273145856 | bytes 6357056 | tf_op jit(solution)/shard_map/while/body/tre,tce->trc/dot_general | solution.py:92
  180.1 2.2 fusion.84
  185.8 7.0 %collective-permute-start.5 = (f32[4096]{0:T(1024)S(1)}, f32[4096]{0:T(1024)S(1)}, u32[]{:S(2)}, u32[]{:S(2)}) collective-permute-start(f32[4096]{0:T(1024)S(1)} %get-tuple-element.216), channel_id=1, source_target_pairs={{0,1},{1,2},{2,3},{3,4},{4,5},{5,6},{6,7},{7,8},{8,9},{9,10},{10,1... | collective-permute-start | bytes 49160 | tf_op jit(solution)/shard_map/ppermute | solution.py:18
  193.8 7.6 %collective-permute-start.6 = (f32[4096]{0:T(1024)S(1)}, f32[4096]{0:T(1024)S(1)}, u32[]{:S(2)}, u32[]{:S(2)}) collective-permute-start(f32[4096]{0:T(1024)S(1)} %subtract_multiply_fusion.1), channel_id=1, source_target_pairs={{0,1},{1,2},{2,3},{3,4},{4,5},{5,6},{6,7},{7,8},{8,9},{9,10},{10,1... | collective-permute-start | bytes 49160 | tf_op jit(solution)/shard_map/ppermute | solution.py:18
  201.4 2.0 collective-permute-start.7
  203.4 6.4 %collective-permute-done.7 = f32[4096]{0:T(1024)S(1)} collective-permute-done((f32[4096]{0:T(1024)S(1)}, f32[4096]{0:T(1024)S(1)}, u32[]{:S(2)}, u32[]{:S(2)}) %collective-permute-start.7) | collective-permute-done | bytes 16416 | tf_op jit(solution)/shard_map/ppermute | solution.py:18
  209.8 111.2 %while.33 = (s32[]{:T(128)}, f32[32,128]{1,0:T(8,128)S(1)}, f32[32,128]{1,0:T(8,128)S(1)}, f32[96,128]{1,0:T(8,128)S(1)}, f32[96,128]{1,0:T(8,128)S(1)}, /*index...) while((s32[]{:T(128)}, f32[32,128]{1,0:T(8,128)S(1)}, ...), condition=%wide.region_19.22_spmd, body=%wide.region_12.0_spmd.sunk | while | flops 277935392 | bytes 13577027 | solution.py:122
  211.4 4.8 %gather_fusion.3 = bf16[32,128,256]{2,1,0:T(8,128)(2,1)} fusion(bf16[96,128,256]{2,1,0:T(8,128)(2,1)} %get-tuple-element.493, s32[1024]{0:T(1024)S(1)} %pad_clamp_fusion.5), kind=kCustom, calls=%fused_computation.5.clone.clone.1 | custom fusion | bytes 4194432 | tf_op jit(solution)/shard_map/while/body/jit(_take)/gather | solution.py:91
  216.2 3.7 %bitcast_reduce_fusion.7 = (f32[32,128]{1,0:T(8,128)S(1)}, f32[32,128]{1,0:T(8,128)S(1)}, f32[32,128,128]{2,1,0:T(8,128)S(1)}) fusion(f32[32,128]{1,0:T(8,128)S(1)} %bitcast.125, f32[32,128]{1,0:T(8,128)S(1)} %broadcast_select_fusion.13, pred[32]{0:T(512)(128)(4,1)S(1)} %dynamic-slice_bitcast_fusion.5, ...), kind=kOutput, calls=%fused_computation.52.clone.1 | convolution fusion | flops 273145856 | bytes 6357056 | tf_op jit(solution)/shard_map/while/body/tre,tce->trc/dot_general | solution.py:92
  220.7 2.2 fusion.89
  225.1 4.8 %gather_fusion.3 = bf16[32,128,256]{2,1,0:T(8,128)(2,1)} fusion(bf16[96,128,256]{2,1,0:T(8,128)(2,1)} %get-tuple-element.493, s32[1024]{0:T(1024)S(1)} %pad_clamp_fusion.5), kind=kCustom, calls=%fused_computation.5.clone.clone.1 | custom fusion | bytes 4194432 | tf_op jit(solution)/shard_map/while/body/jit(_take)/gather | solution.py:91
  230.0 3.7 %bitcast_reduce_fusion.7 = (f32[32,128]{1,0:T(8,128)S(1)}, f32[32,128]{1,0:T(8,128)S(1)}, f32[32,128,128]{2,1,0:T(8,128)S(1)}) fusion(f32[32,128]{1,0:T(8,128)S(1)} %bitcast.125, f32[32,128]{1,0:T(8,128)S(1)} %broadcast_select_fusion.13, pred[32]{0:T(512)(128)(4,1)S(1)} %dynamic-slice_bitcast_fusion.5, ...), kind=kOutput, calls=%fused_computation.52.clone.1 | convolution fusion | flops 273145856 | bytes 6357056 | tf_op jit(solution)/shard_map/while/body/tre,tce->trc/dot_general | solution.py:92
  234.5 2.2 fusion.89
  238.9 4.8 %gather_fusion.3 = bf16[32,128,256]{2,1,0:T(8,128)(2,1)} fusion(bf16[96,128,256]{2,1,0:T(8,128)(2,1)} %get-tuple-element.493, s32[1024]{0:T(1024)S(1)} %pad_clamp_fusion.5), kind=kCustom, calls=%fused_computation.5.clone.clone.1 | custom fusion | bytes 4194432 | tf_op jit(solution)/shard_map/while/body/jit(_take)/gather | solution.py:91
  243.8 3.7 %bitcast_reduce_fusion.7 = (f32[32,128]{1,0:T(8,128)S(1)}, f32[32,128]{1,0:T(8,128)S(1)}, f32[32,128,128]{2,1,0:T(8,128)S(1)}) fusion(f32[32,128]{1,0:T(8,128)S(1)} %bitcast.125, f32[32,128]{1,0:T(8,128)S(1)} %broadcast_select_fusion.13, pred[32]{0:T(512)(128)(4,1)S(1)} %dynamic-slice_bitcast_fusion.5, ...), kind=kOutput, calls=%fused_computation.52.clone.1 | convolution fusion | flops 273145856 | bytes 6357056 | tf_op jit(solution)/shard_map/while/body/tre,tce->trc/dot_general | solution.py:92
  248.3 2.2 fusion.89
  252.7 4.8 %gather_fusion.3 = bf16[32,128,256]{2,1,0:T(8,128)(2,1)} fusion(bf16[96,128,256]{2,1,0:T(8,128)(2,1)} %get-tuple-element.493, s32[1024]{0:T(1024)S(1)} %pad_clamp_fusion.5), kind=kCustom, calls=%fused_computation.5.clone.clone.1 | custom fusion | bytes 4194432 | tf_op jit(solution)/shard_map/while/body/jit(_take)/gather | solution.py:91
  257.5 3.7 %bitcast_reduce_fusion.7 = (f32[32,128]{1,0:T(8,128)S(1)}, f32[32,128]{1,0:T(8,128)S(1)}, f32[32,128,128]{2,1,0:T(8,128)S(1)}) fusion(f32[32,128]{1,0:T(8,128)S(1)} %bitcast.125, f32[32,128]{1,0:T(8,128)S(1)} %broadcast_select_fusion.13, pred[32]{0:T(512)(128)(4,1)S(1)} %dynamic-slice_bitcast_fusion.5, ...), kind=kOutput, calls=%fused_computation.52.clone.1 | convolution fusion | flops 273145856 | bytes 6357056 | tf_op jit(solution)/shard_map/while/body/tre,tce->trc/dot_general | solution.py:92
  262.1 2.2 fusion.89
  266.5 4.8 %gather_fusion.3 = bf16[32,128,256]{2,1,0:T(8,128)(2,1)} fusion(bf16[96,128,256]{2,1,0:T(8,128)(2,1)} %get-tuple-element.493, s32[1024]{0:T(1024)S(1)} %pad_clamp_fusion.5), kind=kCustom, calls=%fused_computation.5.clone.clone.1 | custom fusion | bytes 4194432 | tf_op jit(solution)/shard_map/while/body/jit(_take)/gather | solution.py:91
  271.3 3.7 %bitcast_reduce_fusion.7 = (f32[32,128]{1,0:T(8,128)S(1)}, f32[32,128]{1,0:T(8,128)S(1)}, f32[32,128,128]{2,1,0:T(8,128)S(1)}) fusion(f32[32,128]{1,0:T(8,128)S(1)} %bitcast.125, f32[32,128]{1,0:T(8,128)S(1)} %broadcast_select_fusion.13, pred[32]{0:T(512)(128)(4,1)S(1)} %dynamic-slice_bitcast_fusion.5, ...), kind=kOutput, calls=%fused_computation.52.clone.1 | convolution fusion | flops 273145856 | bytes 6357056 | tf_op jit(solution)/shard_map/while/body/tre,tce->trc/dot_general | solution.py:92
  275.9 2.2 fusion.89
  280.3 4.8 %gather_fusion.3 = bf16[32,128,256]{2,1,0:T(8,128)(2,1)} fusion(bf16[96,128,256]{2,1,0:T(8,128)(2,1)} %get-tuple-element.493, s32[1024]{0:T(1024)S(1)} %pad_clamp_fusion.5), kind=kCustom, calls=%fused_computation.5.clone.clone.1 | custom fusion | bytes 4194432 | tf_op jit(solution)/shard_map/while/body/jit(_take)/gather | solution.py:91
  285.1 3.7 %bitcast_reduce_fusion.7 = (f32[32,128]{1,0:T(8,128)S(1)}, f32[32,128]{1,0:T(8,128)S(1)}, f32[32,128,128]{2,1,0:T(8,128)S(1)}) fusion(f32[32,128]{1,0:T(8,128)S(1)} %bitcast.125, f32[32,128]{1,0:T(8,128)S(1)} %broadcast_select_fusion.13, pred[32]{0:T(512)(128)(4,1)S(1)} %dynamic-slice_bitcast_fusion.5, ...), kind=kOutput, calls=%fused_computation.52.clone.1 | convolution fusion | flops 273145856 | bytes 6357056 | tf_op jit(solution)/shard_map/while/body/tre,tce->trc/dot_general | solution.py:92
  289.7 2.2 fusion.89
  294.1 4.8 %gather_fusion.3 = bf16[32,128,256]{2,1,0:T(8,128)(2,1)} fusion(bf16[96,128,256]{2,1,0:T(8,128)(2,1)} %get-tuple-element.493, s32[1024]{0:T(1024)S(1)} %pad_clamp_fusion.5), kind=kCustom, calls=%fused_computation.5.clone.clone.1 | custom fusion | bytes 4194432 | tf_op jit(solution)/shard_map/while/body/jit(_take)/gather | solution.py:91
  298.9 3.7 %bitcast_reduce_fusion.7 = (f32[32,128]{1,0:T(8,128)S(1)}, f32[32,128]{1,0:T(8,128)S(1)}, f32[32,128,128]{2,1,0:T(8,128)S(1)}) fusion(f32[32,128]{1,0:T(8,128)S(1)} %bitcast.125, f32[32,128]{1,0:T(8,128)S(1)} %broadcast_select_fusion.13, pred[32]{0:T(512)(128)(4,1)S(1)} %dynamic-slice_bitcast_fusion.5, ...), kind=kOutput, calls=%fused_computation.52.clone.1 | convolution fusion | flops 273145856 | bytes 6357056 | tf_op jit(solution)/shard_map/while/body/tre,tce->trc/dot_general | solution.py:92
  303.5 2.2 fusion.89
  307.9 4.8 %gather_fusion.3 = bf16[32,128,256]{2,1,0:T(8,128)(2,1)} fusion(bf16[96,128,256]{2,1,0:T(8,128)(2,1)} %get-tuple-element.493, s32[1024]{0:T(1024)S(1)} %pad_clamp_fusion.5), kind=kCustom, calls=%fused_computation.5.clone.clone.1 | custom fusion | bytes 4194432 | tf_op jit(solution)/shard_map/while/body/jit(_take)/gather | solution.py:91
  312.7 3.7 %bitcast_reduce_fusion.7 = (f32[32,128]{1,0:T(8,128)S(1)}, f32[32,128]{1,0:T(8,128)S(1)}, f32[32,128,128]{2,1,0:T(8,128)S(1)}) fusion(f32[32,128]{1,0:T(8,128)S(1)} %bitcast.125, f32[32,128]{1,0:T(8,128)S(1)} %broadcast_select_fusion.13, pred[32]{0:T(512)(128)(4,1)S(1)} %dynamic-slice_bitcast_fusion.5, ...), kind=kOutput, calls=%fused_computation.52.clone.1 | convolution fusion | flops 273145856 | bytes 6357056 | tf_op jit(solution)/shard_map/while/body/tre,tce->trc/dot_general | solution.py:92
  317.3 2.2 fusion.89
  323.0 7.0 %collective-permute-start.9 = (f32[4096]{0:T(1024)S(1)}, f32[4096]{0:T(1024)S(1)}, u32[]{:S(2)}, u32[]{:S(2)}) collective-permute-start(f32[4096]{0:T(1024)S(1)} %get-tuple-element.213), channel_id=1, source_target_pairs={{0,1},{1,2},{2,3},{3,4},{4,5},{5,6},{6,7},{7,8},{8,9},{9,10},{10,1... | collective-permute-start | bytes 49160 | tf_op jit(solution)/shard_map/ppermute | solution.py:18
  (259 shorter events, 47.6 us)
Async XLA Ops:
  12.7 30.6 %collective-permute-start = (f32[4096]{0:T(1024)S(1)}, f32[4096]{0:T(1024)S(1)}, u32[]{:S(2)}, u32[]{:S(2)}) collective-permute-start(f32[4096]{0:T(1024)S(1)} %select_reduce_fusion), channel_id=1, source_target_pairs={{0,1},{1,2},{2,3},{3,4},{4,5},{5,6},{6,7},{7,8},{8,9},{9,10},{10,1... | collective-permute-start | bytes 49160 | tf_op jit(solution)/shard_map/ppermute | solution.py:18
  17.7 25.6 %collective-permute-start.1 = (f32[4096]{0:T(1024)S(1)}, f32[4096]{0:T(1024)S(1)}, u32[]{:S(2)}, u32[]{:S(2)}) collective-permute-start(f32[4096]{0:T(1024)S(1)} %select_reduce_fusion), channel_id=1, source_target_pairs={{1,0},{2,1},{3,2},{4,3},{5,4},{6,5},{7,6},{8,7},{9,8},{10,9},{11,1... | collective-permute-start | bytes 49160 | tf_op jit(solution)/shard_map/ppermute | solution.py:18
  19.7 30.3 %collective-permute-start.2 = (bf16[4096,256]{1,0:T(8,128)(2,1)}, bf16[4096,256]{1,0:T(8,128)(2,1)S(1)}, u32[]{:S(2)}, u32[]{:S(2)}) collective-permute-start(bf16[4096,256]{1,0:T(8,128)(2,1)} %param.17), channel_id=1, source_target_pairs={{0,1},{1,2},{2,3},{3,4},{4,5},{5,6},{6,7},{7,8},{8,9},{9,10},{10,1... | collective-permute-start | bytes 6291464 | tf_op jit(solution)/shard_map/ppermute | solution.py:18
  26.7 31.0 %collective-permute-start.3 = (bf16[4096,256]{1,0:T(8,128)(2,1)}, bf16[4096,256]{1,0:T(8,128)(2,1)}, u32[]{:S(2)}, u32[]{:S(2)}) collective-permute-start(bf16[4096,256]{1,0:T(8,128)(2,1)} %param.17), channel_id=1, source_target_pairs={{1,0},{2,1},{3,2},{4,3},{5,4},{6,5},{7,6},{8,7},{9,8},{10,9},{11,1... | collective-permute-start | bytes 6291464 | tf_op jit(solution)/shard_map/ppermute | solution.py:18
  183.9 9.0 %collective-permute-start.4 = (f32[4096]{0:T(1024)S(1)}, f32[4096]{0:T(1024)S(1)}, u32[]{:S(2)}, u32[]{:S(2)}) collective-permute-start(f32[4096]{0:T(1024)S(1)} %get-tuple-element.217), channel_id=1, source_target_pairs={{1,0},{2,1},{3,2},{4,3},{5,4},{6,5},{7,6},{8,7},{9,8},{10,9},{11,1... | collective-permute-start | bytes 49160 | tf_op jit(solution)/shard_map/ppermute | solution.py:18
  185.8 7.8 %collective-permute-start.5 = (f32[4096]{0:T(1024)S(1)}, f32[4096]{0:T(1024)S(1)}, u32[]{:S(2)}, u32[]{:S(2)}) collective-permute-start(f32[4096]{0:T(1024)S(1)} %get-tuple-element.216), channel_id=1, source_target_pairs={{0,1},{1,2},{2,3},{3,4},{4,5},{5,6},{6,7},{7,8},{8,9},{9,10},{10,1... | collective-permute-start | bytes 49160 | tf_op jit(solution)/shard_map/ppermute | solution.py:18
  193.8 9.5 %collective-permute-start.6 = (f32[4096]{0:T(1024)S(1)}, f32[4096]{0:T(1024)S(1)}, u32[]{:S(2)}, u32[]{:S(2)}) collective-permute-start(f32[4096]{0:T(1024)S(1)} %subtract_multiply_fusion.1), channel_id=1, source_target_pairs={{0,1},{1,2},{2,3},{3,4},{4,5},{5,6},{6,7},{7,8},{8,9},{9,10},{10,1... | collective-permute-start | bytes 49160 | tf_op jit(solution)/shard_map/ppermute | solution.py:18
  201.4 8.4 %collective-permute-start.7 = (f32[4096]{0:T(1024)S(1)}, f32[4096]{0:T(1024)S(1)}, u32[]{:S(2)}, u32[]{:S(2)}) collective-permute-start(f32[4096]{0:T(1024)S(1)} %subtract_multiply_fusion.1), channel_id=1, source_target_pairs={{1,0},{2,1},{3,2},{4,3},{5,4},{6,5},{7,6},{8,7},{9,8},{10,9},{11,1... | collective-permute-start | bytes 49160 | tf_op jit(solution)/shard_map/ppermute | solution.py:18
  321.0 9.6 %collective-permute-start.8 = (f32[4096]{0:T(1024)S(1)}, f32[4096]{0:T(1024)S(1)}, u32[]{:S(2)}, u32[]{:S(2)}) collective-permute-start(f32[4096]{0:T(1024)S(1)} %get-tuple-element.214), channel_id=1, source_target_pairs={{1,0},{2,1},{3,2},{4,3},{5,4},{6,5},{7,6},{8,7},{9,8},{10,9},{11,1... | collective-permute-start | bytes 49160 | tf_op jit(solution)/shard_map/ppermute | solution.py:18
  323.0 7.8 %collective-permute-start.9 = (f32[4096]{0:T(1024)S(1)}, f32[4096]{0:T(1024)S(1)}, u32[]{:S(2)}, u32[]{:S(2)}) collective-permute-start(f32[4096]{0:T(1024)S(1)} %get-tuple-element.213), channel_id=1, source_target_pairs={{0,1},{1,2},{2,3},{3,4},{4,5},{5,6},{6,7},{7,8},{8,9},{9,10},{10,1... | collective-permute-start | bytes 49160 | tf_op jit(solution)/shard_map/ppermute | solution.py:18
where the time goes:
time: 335 us; the launch traced here: 332 us
  other arithmetic  107 us (32%)
  local copies, waits for them, and re-layouts  86.5 us (26%)
  matrix products  58.6 us (17%)
  starting transfers between devices  43.3 us (13%)
  waiting for transfers between devices  21.9 us (7%)
  loops' own time  13.7 us (4%)
    gather x16, local copies, waits for them, and re-layouts, one_turn(): chosen = jnp.take(window_tiles, picked, axis=0)  76.9 us
    dot_general x16, matrix products, one_turn(): jnp.einsum('tre,tce->trc', source_tiles, chosen, preferred_element_type=j...  58.6 us
    ppermute x10, starting transfers between devices, shifted_2(): return lax.ppermute(block, axis, route)  43.3 us
    reduce_sum x16, other arithmetic, one_turn(): part_total = jnp.sum(jnp.exp(col_terms - part_max[:, None, :]), axis=1)  34.6 us
    reduce_sum x2, other arithmetic, coarse_lookup(): return jnp.sum(jnp.where(matches, coarse_table[None, :], 0.0), axis=1)  24.1 us
    ppermute x10, waiting for transfers between devices, shifted_2(): return lax.ppermute(block, axis, route)  21.9 us
    concatenate x1, other arithmetic, target_window(): return jnp.concatenate(pieces, axis=0)  15 us
    another operation x2, loops' own time, listed_pass(): lax.fori_loop(0, turn_limit, one_turn, starting)  13.7 us
  transfers between devices with their start and end apart: 10, of which 5 were waited for; matrix products, arithmetic and copies ran while one was open for 5% of the time, Pallas kernels for 0%

commit v1 on v0

v1 whole, which is shorter than its diff:
```python
import functools
import math

import jax
import jax.numpy as jnp
from jax import lax
from jax.experimental import pallas as pl
from jax.experimental.pallas import tpu as pltpu
from jax.sharding import PartitionSpec as P

TILE = 128
ITERS = 2
EPSILON = 0.5
NEGATIVE = -1e30
SCALE = 1.0 / (EPSILON * math.log(2.0))
LAST = 12
MESH = pl.DeviceIdType.MESH
VM = pltpu.VMEM
F32 = jnp.float32
SPEC = pl.BlockSpec(memory_space=pltpu.VMEM)
SMEM = pl.BlockSpec(memory_space=pltpu.SMEM)
ANY = pl.BlockSpec(memory_space=pl.ANY)
NT = (((1,), (1,)), ((), ()))
LO, HI = 1e-8, 1e20
FAR = 15.0


def partners(n):
    me = lax.axis_index("row")
    odd = lax.rem(me, 2)
    fast = me + 1 - 2 * odd
    slow = lax.rem(me - 1 + 2 * odd + n, n)
    return me, odd, fast, slow


def place(listed, me, odd, tiles):
    w = listed - (me - 1) * tiles
    turned = jnp.where(w >= 2 * tiles, w - 2 * tiles, jnp.where(w < tiles, w + 2 * tiles, w))
    return jnp.where(odd == 1, w, turned)


def greet(devices):
    barrier = pltpu.get_barrier_semaphore()
    for d in devices:
        pl.semaphore_signal(barrier, inc=1, device_id={"row": d}, device_id_type=MESH)
    pl.semaphore_wait(barrier, len(devices))


def remote(src, dst, sems, i, device):
    send, recv = sems
    return pltpu.make_async_remote_copy(
        src_ref=src,
        dst_ref=dst,
        send_sem=send.at[i],
        recv_sem=recv.at[i],
        device_id={"row": device},
        device_id_type=MESH,
    )


def three(x):
    a = x.astype(jnp.bfloat16)
    rest = x - a.astype(F32)
    b = rest.astype(jnp.bfloat16)
    c = (rest - b.astype(F32)).astype(jnp.bfloat16)
    return a, b, c


def add_up(onehot, parts):
    a, b, c = three(parts)
    dot = lambda y: jnp.dot(onehot, y, preferred_element_type=F32)
    return dot(a) + (dot(b) + dot(c))


def kernel_a(
    n, tiles, maxb,
    bl, bc, src, tgt, scl, tcl, ctab_s, ctab_t,
    k_ref, ra_ref, p1_ref, f0b_ref, g0_ref, x_ref, of_ref, es1_ref, es2_ref, oh_ref, lst_ref,
    ids_ref, tab_ref, f0_ref, oht_ref, ft_ref, send, recv, local,
):
    me, odd, fast, slow = partners(n)
    sems = (send, recv)
    first = tiles - LAST
    greet((fast, slow))
    copies = [
        remote(tcl, ids_ref.at[pl.ds(2 * tiles, tiles)], sems, 0, slow),
        remote(tcl, ids_ref.at[pl.ds(0, tiles)], sems, 1, fast),
        remote(tgt.at[pl.ds(0, first)], es1_ref, sems, 2, slow),
        remote(tgt.at[pl.ds(first, LAST)], es2_ref, sems, 3, slow),
        remote(tgt, of_ref.at[pl.ds(0, tiles)], sems, 4, fast),
    ]
    for c in copies:
        c.start()
    mine = [
        pltpu.make_async_copy(tcl, ids_ref.at[pl.ds(tiles, tiles)], local.at[0]),
        pltpu.make_async_copy(scl, ids_ref.at[pl.ds(3 * tiles, tiles)], local.at[1]),
        pltpu.make_async_copy(src, x_ref, local.at[2]),
        pltpu.make_async_copy(tgt, of_ref.at[pl.ds(tiles, tiles)], local.at[3]),
    ]
    for c in mine:
        c.start()

    for q, tab in enumerate((ctab_s, ctab_t)):
        wide = jnp.concatenate([tab[...], jnp.zeros((TILE - tab.shape[0], TILE), F32)], axis=0)
        turned = jnp.transpose(wide)[:, : tab.shape[0]]
        tab_ref[q] = jnp.concatenate(three(turned), axis=1)

    flat = lax.broadcasted_iota(jnp.int32, (8, TILE), 0) * TILE + lax.broadcasted_iota(
        jnp.int32, (8, TILE), 1
    )
    lane = lax.broadcasted_iota(jnp.int32, (maxb, TILE), 1)
    sub = lax.broadcasted_iota(jnp.int32, (maxb, TILE), 0)

    def order(t, carry):
        lst, count = carry
        active = bc[t]
        where_to = jnp.full((maxb, TILE), -1, jnp.int32)
        for k in range(maxb):
            r = place(bl[t, k], me, odd, tiles)
            on = jnp.where(k < active, 1, 0)
            late = on * jnp.where(r >= 2 * tiles + first, 1, 0)
            lst = lst + jnp.where(flat == count, (t * maxb + k) * late, 0)
            count = count + late
            where_to = jnp.where(sub == k, r * on - (1 - on), where_to)
        oht_ref[pl.ds(pl.multiple_of(t * maxb, maxb), maxb), :] = jnp.where(
            lane == where_to, 1.0, 0.0
        )
        return lst, count

    lst, count = lax.fori_loop(0, tiles, order, (jnp.zeros((8, TILE), jnp.int32), 0))
    lst_ref[...] = jnp.where(flat == 8 * TILE - 1, count, lst)
    oh_ref[...] = jnp.transpose(oht_ref[...]).astype(jnp.bfloat16)

    low = lax.broadcasted_iota(jnp.int32, (TILE, TILE), 0)
    high = lax.broadcasted_iota(jnp.int32, (tiles, TILE), 0)

    def look_up(row, q):
        ids = ids_ref[pl.ds(row, 1), :]
        hit = jnp.where(high == lax.shift_right_logical(ids, 7), 1.0, 0.0).astype(jnp.bfloat16)
        got = jnp.dot(
            tab_ref[q], jnp.concatenate([hit, hit, hit], axis=0), preferred_element_type=F32
        )
        return jnp.sum(jnp.where(low == (ids & 127), got, 0.0), axis=0, keepdims=True)

    mine[0].wait()
    mine[1].wait()

    def own_rows(i, _):
        for u in range(4):
            t = i * 4 + u
            f0_ref[pl.ds(t, 1), :] = look_up(3 * tiles + t, 0)
            g0_ref[pl.ds(tiles + t, 1), :] = look_up(tiles + t, 1)
        return 0

    lax.fori_loop(0, tiles // 4, own_rows, 0)
    ft_ref[...] = jnp.transpose(
        jnp.concatenate([f0_ref[...], jnp.zeros((TILE - tiles, TILE), F32)], axis=0)
    )
    lanes = lax.broadcasted_iota(jnp.int32, (TILE, TILE), 1)

    def spread(i, _):
        for u in range(2):
            t = i * 2 + u
            col = jnp.sum(jnp.where(lanes == t, ft_ref[...], 0.0), axis=1, keepdims=True)
            f0b_ref[t] = jnp.broadcast_to(col, (TILE, TILE))
        return 0

    lax.fori_loop(0, tiles // 2, spread, 0)
    copies[0].wait_recv()
    copies[1].wait_recv()

    def other_rows(i, _):
        for u in range(4):
            t = i * 4 + u
            g0_ref[pl.ds(t, 1), :] = look_up(t, 1)
            g0_ref[pl.ds(2 * tiles + t, 1), :] = look_up(2 * tiles + t, 1)
        return 0

    lax.fori_loop(0, tiles // 4, other_rows, 0)
    mine[2].wait()
    mine[3].wait()
    copies[4].wait_recv()

    def near(t, _):
        x = x_ref[t]
        active = bc[t]
        for k in range(0, maxb, 2):
            ys, bias = [], []
            for u in range(2):
                r = place(bl[t, k + u], me, odd, tiles)
                ys.append(of_ref[jnp.clip(r, 0, 2 * tiles - 1)])
                on = jnp.where(k + u < active, 1, 0) * jnp.where(r < 2 * tiles, 1, 0)
                bias.append(jnp.where(on == 1, 0.0, NEGATIVE).astype(F32))
            s = lax.dot_general(x, jnp.concatenate(ys, axis=0), NT, preferred_element_type=F32)
            for u in range(2):
                part = s[:, u * TILE : (u + 1) * TILE]
                k_ref[t * maxb + k + u] = jnp.exp2(part * SCALE + bias[u])
        return 0

    lax.fori_loop(0, tiles, near, 0)
    copies[2].wait_recv()

    def middle(t, _):
        x = x_ref[t]
        active = bc[t]
        b0 = jnp.exp2(f0b_ref[t] * SCALE)
        rows = jnp.zeros((TILE, TILE), F32)
        cols = []
        for k in range(0, maxb, 2):
            ys, bias, at = [], [], []
            for u in range(2):
                r = place(bl[t, k + u], me, odd, tiles)
                at.append(jnp.clip(r, 0, 3 * tiles - 1))
                inner = r - 2 * tiles
                ys.append(es1_ref[jnp.clip(inner, 0, first - 1)])
                on = (
                    jnp.where(k + u < active, 1, 0)
                    * jnp.where(inner >= 0, 1, 0)
                    * jnp.where(inner < first, 1, 0)
                )
                bias.append(jnp.where(on == 1, 0.0, NEGATIVE).astype(F32))
            s = lax.dot_general(x, jnp.concatenate(ys, axis=0), NT, preferred_element_type=F32)
            for u in range(2):
                part = s[:, u * TILE : (u + 1) * TILE]
                p = t * maxb + k + u
                kv = k_ref[p] + jnp.exp2(part * SCALE + bias[u])
                k_ref[p] = kv
                rows = rows + kv * jnp.exp2(g0_ref[pl.ds(at[u], 1), :] * SCALE)
                cols.append(jnp.sum(kv * b0, axis=0, keepdims=True))
        ra_ref[t] = rows
        p1_ref[pl.ds(pl.multiple_of(t * maxb, maxb), maxb), :] = jnp.concatenate(cols, axis=0)
        return 0

    lax.fori_loop(0, tiles, middle, 0)
    copies[3].wait_recv()
    for c in copies:
        c.wait_send()


def fetch(r, ybuf, of_ref, es1_ref, es2_ref, tiles):
    first = tiles - LAST

    @pl.when(r < 2 * tiles)
    def _():
        ybuf[...] = of_ref[jnp.minimum(r, 2 * tiles - 1)]

    @pl.when((r >= 2 * tiles) & (r < 2 * tiles + first))
    def _():
        ybuf[...] = es1_ref[jnp.clip(r - 2 * tiles, 0, first - 1)]

    @pl.when(r >= 2 * tiles + first)
    def _():
        ybuf[...] = es2_ref[jnp.clip(r - 2 * tiles - first, 0, LAST - 1)]


def kernel_b(
    n, tiles, maxb, log_size,
    bl, bc, lst, k_in, ra_in, p1_in, f0b_ref, g0_ref, x_ref, of_ref, es1_ref, es2_ref, oh_ref,
    k_ref, ra_ref, p1_ref, f1b_ref, c1_ref, c2_ref, bad_ref,
    ybuf, cols,
):
    me, odd, fast, slow = partners(n)
    first = tiles - LAST
    pairs = tiles * maxb
    count = lst[7, TILE - 1]
    wide = 4

    def late(i, _):
        for u in range(wide):
            at = i * wide + u
            ok = at < count
            p = lst[lax.shift_right_logical(at, 7), at & 127]
            t = lax.div(p, maxb)
            r = place(bl[t, lax.rem(p, maxb)], me, odd, tiles)
            r = jnp.clip(r, 0, 3 * tiles - 1)
            y = es2_ref[jnp.clip(r - 2 * tiles - first, 0, LAST - 1)]
            s = lax.dot_general(x_ref[t], y, NT, preferred_element_type=F32)
            kv = jnp.exp2(s * SCALE + jnp.where(ok, 0.0, NEGATIVE).astype(F32))
            b0 = jnp.exp2(f0b_ref[t] * SCALE)
            a0 = jnp.exp2(g0_ref[pl.ds(r, 1), :] * SCALE)
            ra_ref[t] = ra_ref[t] + kv * a0
            p1_ref[pl.ds(p, 1), :] = p1_ref[pl.ds(p, 1), :] + jnp.sum(
                kv * b0, axis=0, keepdims=True
            )
            k_ref[p] = k_ref[p] + kv
        return 0

    lax.fori_loop(0, lax.div(count + wide - 1, wide), late, 0)

    def finish(i, worst):
        for u in range(4):
            t = i * 4 + u
            total = jnp.sum(ra_ref[t], axis=1, keepdims=True)
            worst = jnp.maximum(worst, jnp.where((total >= LO) & (total <= HI), 0.0, 1.0))
            lse = jnp.broadcast_to(jnp.log(total), (TILE, TILE))
            f1b_ref[t] = 0.5 * (f0b_ref[t] + log_size - EPSILON * lse)
        return worst

    worst = lax.fori_loop(0, tiles // 4, finish, jnp.zeros((TILE, 1), F32))
    onehot = oh_ref[...]
    here = jnp.sum(onehot.astype(F32), axis=1, keepdims=True) > 0.5
    total = add_up(onehot, p1_ref[...])
    fits = (total >= LO) & (total <= HI)
    c1_ref[...] = jnp.where(here, jnp.log(total), NEGATIVE)[: 3 * tiles]
    wrong = jnp.where(here & jnp.logical_not(fits), 1.0, 0.0)
    bad = jnp.maximum(jnp.max(worst), jnp.max(wrong))
    bad_ref[...] = jnp.full((8, TILE), bad)
    c2_ref[...] = jnp.full((3 * tiles, TILE), NEGATIVE, F32)

    @pl.when(bad > 0.5)
    def _():
        for c in range(4):
            cols[c] = jnp.full((3 * tiles, TILE), NEGATIVE if c % 2 == 0 else 0.0, F32)

        def column(c, r, terms):
            top = cols[c, pl.ds(r, 1), :]
            now = jnp.maximum(top, jnp.max(terms, axis=0, keepdims=True))
            cols[c + 1, pl.ds(r, 1), :] = cols[c + 1, pl.ds(r, 1), :] * jnp.exp(top - now) + jnp.sum(
                jnp.exp(terms - now), axis=0, keepdims=True
            )
            cols[c, pl.ds(r, 1), :] = now

        def one(t, _):
            x = x_ref[t]
            f0 = f0b_ref[t]

            def slot(k, carry):
                top, total = carry
                r = place(bl[t, k], me, odd, tiles)
                fetch(r, ybuf, of_ref, es1_ref, es2_ref, tiles)
                s = lax.dot_general(x, ybuf[...], NT, preferred_element_type=F32)
                terms = (g0_ref[pl.ds(r, 1), :] + s) / EPSILON
                now = jnp.maximum(top, jnp.max(terms, axis=1, keepdims=True))
                total = total * jnp.exp(top - now) + jnp.sum(
                    jnp.exp(terms - now), axis=1, keepdims=True
                )
                column(0, r, (f0 + s) / EPSILON)
                return now, total

            top, total = lax.fori_loop(
                0, bc[t], slot, (jnp.full((TILE, 1), NEGATIVE, F32), jnp.zeros((TILE, 1), F32))
            )
            lse = jnp.broadcast_to(top + jnp.log(total), (TILE, TILE))
            f1 = 0.5 * (f0 + log_size - EPSILON * lse)
            f1b_ref[t] = f1

            def again(k, _):
                r = place(bl[t, k], me, odd, tiles)
                fetch(r, ybuf, of_ref, es1_ref, es2_ref, tiles)
                s = lax.dot_general(x, ybuf[...], NT, preferred_element_type=F32)
                column(2, r, (f1b_ref[t] + s) / EPSILON)
                return 0

            lax.fori_loop(0, bc[t], again, 0)
            return 0

        lax.fori_loop(0, tiles, one, 0)
        c1_ref[...] = jnp.where(cols[1] > 0, cols[0] + jnp.log(cols[1]), NEGATIVE)
        c2_ref[...] = jnp.where(cols[3] > 0, cols[2] + jnp.log(cols[3]), NEGATIVE)


def merge(*parts):
    top = functools.reduce(jnp.maximum, parts)
    return top + jnp.log(functools.reduce(jnp.add, [jnp.exp(p - top) for p in parts]))


def kernel_f(
    n, tiles, maxb, log_size,
    bl, k_ref, f1b_ref, g0_ref, oh_ref, c1_ref, c2s_ref, bad_ref,
    f2_ref, g2_ref, g1_ref,
    p2_ref, c2_ref, a1_ref, ft_ref, got_f, got_s, got_fs, got_sf, got2_f, got2_s, send, recv,
):
    me, odd, fast, slow = partners(n)
    beyond_fast = lax.rem(fast - 1 + 2 * (1 - odd) + n, n)
    beyond_slow = slow - 1 + 2 * odd
    sems = (send, recv)
    greet((fast, slow, beyond_fast, beyond_slow))
    copies = [
        remote(c1_ref.at[pl.ds(tiles, 2 * tiles)], got_s, sems, 0, slow),
        remote(c1_ref.at[pl.ds(0, tiles)], got_sf, sems, 1, beyond_fast),
        remote(c1_ref.at[pl.ds(2 * tiles, tiles)], got_fs, sems, 2, beyond_slow),
        remote(c1_ref.at[pl.ds(0, 2 * tiles)], got_f, sems, 3, fast),
    ]
    for c in copies:
        c.start()

    def columns(t, _):
        b1 = jnp.exp2(f1b_ref[t] * SCALE)
        p2_ref[pl.ds(pl.multiple_of(t * maxb, maxb), maxb), :] = jnp.concatenate(
            [jnp.sum(k_ref[t * maxb + k] * b1, axis=0, keepdims=True) for k in range(maxb)], axis=0
        )
        return 0

    lax.fori_loop(0, tiles, columns, 0)
    total = add_up(oh_ref[...], p2_ref[...])[: 3 * tiles]
    quick = jnp.where(total > 0, jnp.log(total), NEGATIVE)
    c2_ref[...] = jnp.where(bad_ref[0:1, :] > 0.5, c2s_ref[...], quick)

    for c in copies:
        c.wait_recv()
    own = pl.ds(tiles, tiles)
    front, back = pl.ds(0, tiles), pl.ds(2 * tiles, tiles)
    second = pl.ds(tiles, tiles)
    for part, lse in (
        (front, merge(c1_ref[front, :], got_f[second, :], got_fs[...])),
        (own, merge(c1_ref[own, :], got_f[front, :], got_s[second, :])),
        (back, merge(c1_ref[back, :], got_s[front, :], got_sf[...])),
    ):
        g1 = 0.5 * (g0_ref[part, :] + log_size - EPSILON * lse)
        g1_ref[part, :] = g1
        a1_ref[part, :] = jnp.exp2(g1 * SCALE)
    final = [
        remote(c2_ref.at[back], got2_s, sems, 4, slow),
        remote(c2_ref.at[front], got2_f, sems, 5, fast),
    ]
    for c in final:
        c.start()

    lanes = lax.broadcasted_iota(jnp.int32, (TILE, TILE), 1)
    ft_ref[...] = jnp.zeros((TILE, TILE), F32)

    def rows(t, _):
        total = jnp.zeros((TILE, TILE), F32)
        for k in range(maxb):
            r = jnp.clip(place(bl[t, k], me, odd, tiles), 0, 3 * tiles - 1)
            total = total + k_ref[t * maxb + k] * a1_ref[pl.ds(r, 1), :]
        total = jnp.sum(total, axis=1, keepdims=True)
        fits = (total >= LO) & (total <= HI)
        lse = jnp.broadcast_to(jnp.log(jnp.where(fits, total, jnp.nan)), (TILE, TILE))
        f2 = 0.5 * (f1b_ref[t] + log_size - EPSILON * lse)
        ft_ref[...] = jnp.where(lanes == t, f2, ft_ref[...])
        return 0

    lax.fori_loop(0, tiles, rows, 0)
    f2_ref[...] = jnp.transpose(ft_ref[...])[:tiles]
    for c in final:
        c.wait_recv()
    lse = merge(c2_ref[own, :], got2_f[...], got2_s[...])
    g2_ref[...] = 0.5 * (g1_ref[own, :] + log_size - EPSILON * lse)
    for c in copies + final:
        c.wait_send()


def kernel_g(
    n, tiles, maxb, log_size,
    bl, bc, f2_in, g2_in, g1_ref, bad_ref, f1b_ref, x_ref, of_ref, es1_ref, es2_ref,
    f2_ref, g2_ref, ft_ref, ybuf,
):
    me, odd, fast, slow = partners(n)
    f2 = f2_in[...]
    f2_ref[...] = f2
    g2_ref[...] = g2_in[...]
    odd_one = jnp.where(f2 == f2, 0.0, 1.0)
    bad = jnp.maximum(
        jnp.maximum(jnp.max(odd_one), jnp.max(bad_ref[...])),
        jnp.max(jnp.where(jnp.abs(g1_ref[...]) <= FAR, 0.0, 1.0)),
    )

    @pl.when(bad > 0.5)
    def _():
        lanes = lax.broadcasted_iota(jnp.int32, (TILE, TILE), 1)
        ft_ref[...] = jnp.zeros((TILE, TILE), F32)

        def one(t, _):
            x = x_ref[t]

            def slot(k, carry):
                top, total = carry
                r = place(bl[t, k], me, odd, tiles)
                fetch(r, ybuf, of_ref, es1_ref, es2_ref, tiles)
                s = lax.dot_general(x, ybuf[...], NT, preferred_element_type=F32)
                terms = (g1_ref[pl.ds(r, 1), :] + s) / EPSILON
                now = jnp.maximum(top, jnp.max(terms, axis=1, keepdims=True))
                total = total * jnp.exp(top - now) + jnp.sum(
                    jnp.exp(terms - now), axis=1, keepdims=True
                )
                return now, total

            top, total = lax.fori_loop(
                0, bc[t], slot, (jnp.full((TILE, 1), NEGATIVE, F32), jnp.zeros((TILE, 1), F32))
            )
            lse = jnp.broadcast_to(top + jnp.log(total), (TILE, TILE))
            f2 = 0.5 * (f1b_ref[t] + log_size - EPSILON * lse)
            ft_ref[...] = jnp.where(lanes == t, f2, ft_ref[...])
            return 0

        lax.fori_loop(0, tiles, one, 0)
        f2_ref[...] = jnp.transpose(ft_ref[...])[:tiles]


def shards(n, src, tgt, scl, tcl, cs, ct, bl, bc):
    rows, width = src.shape
    tiles = rows // TILE
    maxb = bl.shape[1]
    first = tiles - LAST
    log_size = EPSILON * math.log(rows * n)
    bf = jnp.bfloat16
    cost = lambda flops: pl.CostEstimate(flops=flops, bytes_accessed=1 << 23, transcendentals=0)
    flops = 2 * tiles * maxb * TILE * TILE * width
    by_tile = lambda a: a.reshape(tiles, TILE, width)
    rows_of = lambda a: a.reshape(tiles, TILE)
    table = lambda a: a.reshape(a.shape[0] // TILE, TILE)
    hold = VM if KEEP else jax.ShapeDtypeStruct
    k, ra, p1, f0b, g0, x, of, es1, es2, oh, lst = pl.pallas_call(
        functools.partial(kernel_a, n, tiles, maxb),
        out_shape=(
            hold((tiles * maxb, TILE, TILE), F32),
            hold((tiles, TILE, TILE), F32),
            hold((tiles * maxb, TILE), F32),
            hold((tiles, TILE, TILE), F32),
            hold((3 * tiles, TILE), F32),
            hold((tiles, TILE, width), bf),
            hold((2 * tiles, TILE, width), bf),
            hold((first, TILE, width), bf),
            hold((LAST, TILE, width), bf),
            hold((TILE, tiles * maxb), bf),
            jax.ShapeDtypeStruct((8, TILE), jnp.int32),
        ),
        in_specs=[SMEM, SMEM, ANY, ANY, ANY, ANY, SPEC, SPEC],
        out_specs=(SPEC,) * 11,
        scratch_shapes=[
            VM((4 * tiles, TILE), jnp.int32),
            VM((2, TILE, 3 * tiles), bf),
            VM((tiles, TILE), F32),
            VM((tiles * maxb, TILE), F32),
            VM((TILE, TILE), F32),
            pltpu.SemaphoreType.DMA((5,)),
            pltpu.SemaphoreType.DMA((5,)),
            pltpu.SemaphoreType.DMA((4,)),
        ],
        compiler_params=pltpu.CompilerParams(
            collective_id=0, has_side_effects=True, vmem_limit_bytes=LIMIT
        ),
        cost_estimate=cost(2 * flops),
        name="exchange",
    )(bl, bc, by_tile(src), by_tile(tgt), rows_of(scl), rows_of(tcl), table(cs), table(ct))

    k, ra, p1, f1b, c1, c2s, bad = pl.pallas_call(
        functools.partial(kernel_b, n, tiles, maxb, log_size),
        out_shape=(
            hold((tiles * maxb, TILE, TILE), F32),
            hold((tiles, TILE, TILE), F32),
            hold((tiles * maxb, TILE), F32),
            hold((tiles, TILE, TILE), F32),
            hold((3 * tiles, TILE), F32),
            hold((3 * tiles, TILE), F32),
            hold((8, TILE), F32),
        ),
        in_specs=[SMEM, SMEM, SMEM] + [SPEC] * 10,
        out_specs=(SPEC,) * 7,
        scratch_shapes=[
            VM((TILE, width), bf),
            VM((4, 3 * tiles, TILE), F32),
        ],
        input_output_aliases={3: 0, 4: 1, 5: 2},
        compiler_params=pltpu.CompilerParams(vmem_limit_bytes=LIMIT),
        cost_estimate=cost(flops),
        name="last_pairs",
    )(bl, bc, lst, k, ra, p1, f0b, g0, x, of, es1, es2, oh)

    f2, g2, g1 = pl.pallas_call(
        functools.partial(kernel_f, n, tiles, maxb, log_size),
        out_shape=(
            hold((tiles, TILE), F32),
            hold((tiles, TILE), F32),
            hold((3 * tiles, TILE), F32),
        ),
        in_specs=[SMEM] + [SPEC] * 7,
        out_specs=(SPEC,) * 3,
        scratch_shapes=[
            VM((tiles * maxb, TILE), F32),
            VM((3 * tiles, TILE), F32),
            VM((3 * tiles, TILE), F32),
            VM((TILE, TILE), F32),
            VM((2 * tiles, TILE), F32),
            VM((2 * tiles, TILE), F32),
            VM((tiles, TILE), F32),
            VM((tiles, TILE), F32),
            VM((tiles, TILE), F32),
            VM((tiles, TILE), F32),
            pltpu.SemaphoreType.DMA((6,)),
            pltpu.SemaphoreType.DMA((6,)),
        ],
        compiler_params=pltpu.CompilerParams(
            collective_id=1, has_side_effects=True, vmem_limit_bytes=LIMIT
        ),
        cost_estimate=cost(flops),
        name="potentials",
    )(bl, k, f1b, g0, oh, c1, c2s, bad)

    f2, g2 = pl.pallas_call(
        functools.partial(kernel_g, n, tiles, maxb, log_size),
        out_shape=(jax.ShapeDtypeStruct((tiles, TILE), F32),) * 2,
        in_specs=[SMEM, SMEM] + [SPEC] * 9,
        out_specs=(SPEC,) * 2,
        scratch_shapes=[VM((TILE, TILE), F32), VM((TILE, width), bf)],
        compiler_params=pltpu.CompilerParams(vmem_limit_bytes=LIMIT),
        cost_estimate=cost(flops),
        name="guard",
    )(bl, bc, f2, g2, g1, bad, f1b, x, of, es1, es2)
    return f2.reshape(rows), g2.reshape(rows)


KEEP = True
LIMIT = 14 << 20


def solution(mesh):
    both = P(("grp", "row"))
    wide = P(("grp", "row"), None)
    return jax.shard_map(
        functools.partial(shards, mesh.shape["row"]),
        mesh=mesh,
        in_specs=(wide, wide, both, both, P("grp"), P("grp"), wide, both),
        out_specs=(both, both),
        check_vma=False,
    )
```

time: 335 us -> 314 us (0.937)
  the two profiles are of different devices: /device:TPU:575 before, /device:TPU:640 now
where the time goes in v1:
time: 314 us
  Pallas kernels  305 us (97%)
  local copies, waits for them, and re-layouts  7.48 us (2%)
    pallas_call x1, Pallas kernels, shards(): pl.pallas_call(functools.partial(kernel_b, n, tiles, maxb, log_size), out...  153 us
    pallas_call x1, Pallas kernels, shards(): pl.pallas_call(functools.partial(kernel_g, n, tiles, maxb, log_size), out...  93.5 us
    pallas_call x1, Pallas kernels, shards(): pl.pallas_call(functools.partial(kernel_a, n, tiles, maxb), out_shape=(ho...  45.9 us
    pallas_call x1, Pallas kernels, shards(): pl.pallas_call(functools.partial(kernel_f, n, tiles, maxb, log_size), out...  12.9 us
    unnamed x21, local copies, waits for them, and re-layouts  7.48 us

profile of v1, /device:TPU:640, one launch (start us, length us, event | category | flops | bytes accessed | tf_op | source)
XLA Modules:
  0.0 313.5 jit_solution(280890346876537532)
XLA Ops:
  0.6 0.8 copy.16.bl
  1.4 0.0 copy-start.2
  1.4 0.7 copy-done.2
  2.0 0.0 copy-start.4
  2.0 1.6 copy-done.4
  3.6 0.0 copy-start.5
  3.6 1.6 copy-done.5
  5.2 0.0 copy-start.6
  5.2 0.7 copy-done.6
  5.9 0.0 copy-start.7
  6.0 0.7 copy-done.7
  6.7 0.0 copy-start.8
  6.7 0.7 copy-done.8
  7.4 0.0 copy-start.9
  7.4 0.7 copy-done.9
  8.1 45.9 %exchange.1 = (f32[256,128,128]{2,1,0:T(8,128)S(1)}, f32[32,128,128]{2,1,0:T(8,128)S(1)}, f32[256,128]{1,0:T(8,128)S(1)}, f32[32,128,128]{2,1,0:T(8,128)S(1)}, f...) custom-call(s32[32,8]{1,0:T(8,128)S(1)} %copy.16.bl, ...), custom_call_target="tpu_custom_call" | custom-call | flops 4294967296 | bytes 8388608 | tf_op jit(solution)/shard_map/exchange/pallas_call | solution.py:504
  54.0 0.0 copy-start
  54.0 153.1 %last_pairs.1 = (f32[256,128,128]{2,1,0:T(8,128)S(1)}, f32[32,128,128]{2,1,0:T(8,128)S(1)}, f32[256,128]{1,0:T(8,128)S(1)}, f32[32,128,128]{2,1,0:T(8,128)S(1)},...) custom-call(s32[32,8]{1,0:T(8,128)S(1)} %copy.16.bl, ...), custom_call_target="tpu_custom_call", output_to_operand_aliasing={{0}: (3, {}), {1}: (4, {}), {2}: (5, {})} | custom-call | flops 2147483648 | bytes 8388608 | tf_op jit(solution)/shard_map/last_pairs/pallas_call | solution.py:538
  207.1 0.0 copy-done
  207.1 0.0 copy-start.1
  207.1 0.0 copy-start.3
  207.1 12.9 %potentials.1 = (f32[32,128]{1,0:T(8,128)S(1)}, f32[32,128]{1,0:T(8,128)S(1)}, f32[96,128]{1,0:T(8,128)S(1)}) custom-call(s32[32,8]{1,0:T(8,128)S(1)} %copy.16.bl, f32[256,128,128]{2,1,0:T(8,128)S(1)} %get-tuple-element.34.k_ref, f32[32,128,128]{2,1,0:T(8,128)S(1)} %get-tuple-element.35.f1b_ref, f32[96,128]{1,0:T(8,128)S(1)} %get-tuple-element.28.g0_ref, ...), custom_call_target="tpu_custom_call" | custom-call | flops 2147483648 | bytes 8388608 | tf_op jit(solution)/shard_map/potentials/pallas_call | solution.py:561
  220.0 0.0 copy-done.1
  220.0 0.0 copy-done.3
  220.0 93.5 %guard.1 = (f32[32,128]{1,0:T(8,128)}, f32[32,128]{1,0:T(8,128)}) custom-call(s32[32,8]{1,0:T(8,128)S(1)} %copy.16.bl, s32[32]{0:T(128)S(1)} %copy-done.3, f32[32,128]{1,0:T(8,128)S(1)} %get-tuple-element.39.f2_in, f32[32,128]{1,0:T(8,128)S(1)} %get-tuple-element.40.g2_in, f32[96,128]{1,0:T(8,128)S(1)} %get-tuple-element.41.g1_ref, ...), custom_call_target="tpu_custom_call" | custom-call | flops 2147483648 | bytes 8388608 | tf_op jit(solution)/shard_map/guard/pallas_call | solution.py:591
Async XLA Ops:
  1.4 0.7 copy-start.2
  2.0 1.6 copy-start.4
  3.6 1.6 copy-start.5
  5.2 0.7 copy-start.6
  5.9 0.7 copy-start.7
  6.7 0.7 copy-start.8
  7.4 0.7 copy-start.9
  54.0 153.1 %copy-start = (bf16[32,128,256]{2,1,0:T(8,128)(2,1)}, bf16[32,128,256]{2,1,0:T(8,128)(2,1)S(1)}, u32[]{:S(2)}) copy-start(bf16[32,128,256]{2,1,0:T(8,128)(2,1)S(1)} %get-tuple-element.29.x_ref) | copy-start | bytes 6291460
  207.1 12.9 %copy-start.1 = (bf16[32,128,256]{2,1,0:T(8,128)(2,1)S(1)}, bf16[32,128,256]{2,1,0:T(8,128)(2,1)}, u32[]{:S(2)}) copy-start(bf16[32,128,256]{2,1,0:T(8,128)(2,1)} %copy-done) | copy-start | bytes 6291460
  207.1 12.9 %copy-start.3 = (s32[32]{0:T(128)S(1)}, s32[32]{0:T(128)}, u32[]{:S(2)}) copy-start(s32[32]{0:T(128)} %bc.5) | copy-start | bytes 388

commit v2 on v1

v2 whole, which is shorter than its diff:
```python
import functools
import math

import jax
import jax.numpy as jnp
from jax import lax
from jax.experimental import pallas as pl
from jax.experimental.pallas import tpu as pltpu
from jax.sharding import PartitionSpec as P

TILE = 128
ITERS = 2
EPSILON = 0.5
NEGATIVE = -1e30
SCALE = 1.0 / (EPSILON * math.log(2.0))
WIDE = 8
MESH = pl.DeviceIdType.MESH
VM = pltpu.VMEM
F32 = jnp.float32
SPEC = pl.BlockSpec(memory_space=pltpu.VMEM)
SMEM = pl.BlockSpec(memory_space=pltpu.SMEM)
ANY = pl.BlockSpec(memory_space=pl.ANY)
FAR_MEM = pl.BlockSpec(memory_space=pltpu.HBM)
NT = (((1,), (1,)), ((), ()))
LO, HI = 1e-8, 1e20
FAR = 15.0


def partners(n):
    me = lax.axis_index("row")
    odd = lax.rem(me, 2)
    slow = me - 1 + 2 * odd
    return me, odd, me + 1 - 2 * odd, slow, (slow >= 0) & (slow < n)


def place(listed, me, odd, tiles):
    w = listed - (me - 1) * tiles
    turned = jnp.where(w >= 2 * tiles, w - 2 * tiles, jnp.where(w < tiles, w + 2 * tiles, w))
    return jnp.where(odd == 1, w, turned)


def greet(device):
    pl.semaphore_signal(
        pltpu.get_barrier_semaphore(), inc=1, device_id={"row": device}, device_id_type=MESH
    )


def remote(src, dst, sems, i, device):
    send, recv = sems
    return pltpu.make_async_remote_copy(
        src_ref=src,
        dst_ref=dst,
        send_sem=send.at[i],
        recv_sem=recv.at[i],
        device_id={"row": device},
        device_id_type=MESH,
    )


def three(x):
    a = x.astype(jnp.bfloat16)
    rest = x - a.astype(F32)
    b = rest.astype(jnp.bfloat16)
    c = (rest - b.astype(F32)).astype(jnp.bfloat16)
    return a, b, c


def add_up(onehot, parts):
    a, b, c = three(parts)
    dot = lambda y: jnp.dot(onehot, y, preferred_element_type=F32)
    return dot(a) + (dot(b) + dot(c))


def kernel_a(
    n, tiles, maxb,
    bl_hbm, bc_hbm, src, tgt, scl, tcl, cs_hbm, ct_hbm,
    ft_ref, g0_ref, a0_ref, x_ref, of_ref, oh_ref, lst_ref,
    bl, bc, ids_ref, ctab_ref, tab_ref, f0_ref, oht_ref, send, recv, local,
):
    me, odd, fast, slow, has_slow = partners(n)
    sems = (send, recv)
    here = [
        pltpu.make_async_copy(bl_hbm, bl, local.at[0]),
        pltpu.make_async_copy(bc_hbm, bc, local.at[1]),
        pltpu.make_async_copy(cs_hbm, ctab_ref.at[0], local.at[2]),
        pltpu.make_async_copy(ct_hbm, ctab_ref.at[1], local.at[3]),
        pltpu.make_async_copy(tcl, ids_ref.at[pl.ds(tiles, tiles)], local.at[4]),
        pltpu.make_async_copy(scl, ids_ref.at[pl.ds(3 * tiles, tiles)], local.at[5]),
        pltpu.make_async_copy(tgt, of_ref.at[pl.ds(tiles, tiles)], local.at[6]),
        pltpu.make_async_copy(src, x_ref, local.at[7]),
    ]
    past_fast, past_slow = fast + 1 - 2 * odd, slow - 1 + 2 * odd
    has_past = (past_fast >= 0) & (past_fast < n)
    greet(fast)

    @pl.when(has_past)
    def _():
        greet(past_fast)

    @pl.when(has_slow)
    def _():
        greet(past_slow)

    for c in here:
        c.start()
    pl.semaphore_wait(
        pltpu.get_barrier_semaphore(), 1 + jnp.where(has_slow, 1, 0) + jnp.where(has_past, 1, 0)
    )
    near = [
        remote(tcl, ids_ref.at[pl.ds(0, tiles)], sems, 0, fast),
        remote(tgt, of_ref.at[pl.ds(0, tiles)], sems, 1, fast),
    ]
    onward = remote(
        ids_ref.at[pl.ds(0, tiles)], ids_ref.at[pl.ds(2 * tiles, tiles)], sems, 2, past_fast
    )
    for c in near:
        c.start()
    for c in here[:4]:
        c.wait()

    for q in range(2):
        wide = jnp.concatenate([ctab_ref[q], jnp.zeros((TILE - tiles, TILE), F32)], axis=0)
        tab_ref[q] = jnp.concatenate(three(jnp.transpose(wide)[:, :tiles]), axis=1)

    pairs = tiles * maxb
    flat = lax.broadcasted_iota(jnp.int32, (16, TILE), 0) * TILE + lax.broadcasted_iota(
        jnp.int32, (16, TILE), 1
    )
    lane = lax.broadcasted_iota(jnp.int32, (maxb, TILE), 1)
    sub = lax.broadcasted_iota(jnp.int32, (maxb, TILE), 0)

    def order(t, carry):
        lst, n0, n1, n2 = carry
        active = bc[t]
        lst = jnp.where(flat == 9 * TILE + t, active, lst)
        where_to = jnp.full((maxb, TILE), -1, jnp.int32)
        for k in range(maxb):
            p = t * maxb + k
            r = place(bl[k, t], me, odd, tiles)
            on = jnp.where(k < active, 1, 0)
            back = jnp.where(r >= 2 * tiles, on, 0)
            front = on - back
            at = jnp.where(on == 0, 2 * pairs + n2, jnp.where(back == 1, pairs + n1, n0))
            lst = jnp.where(flat == at, r * (2 * pairs) + p, lst)
            lst = jnp.where(flat == 3 * pairs + p, r, lst)
            n0, n1, n2 = n0 + front, n1 + back, n2 + 1 - on
            where_to = jnp.where(sub == k, r * on - (1 - on), where_to)
        oht_ref[pl.ds(pl.multiple_of(t * maxb, maxb), maxb), :] = jnp.where(
            lane == where_to, 1.0, 0.0
        )
        return lst, n0, n1, n2

    lst, n0, n1, n2 = lax.fori_loop(
        0, tiles, order, (jnp.full((16, TILE), pairs, jnp.int32), 0, 0, 0)
    )
    for c, count in enumerate((n0, n1, n2)):
        lst = jnp.where(flat == 8 * TILE + c, count, lst)
    lst_ref[...] = lst
    oh_ref[...] = jnp.transpose(oht_ref[...]).astype(jnp.bfloat16)

    low = lax.broadcasted_iota(jnp.int32, (TILE, TILE), 0)
    high = lax.broadcasted_iota(jnp.int32, (tiles, TILE), 0)

    low2 = jnp.concatenate([low, low], axis=1)
    high2 = jnp.concatenate([high, high], axis=1)

    def look_up(row, q, out, at):
        ids = jnp.concatenate([ids_ref[pl.ds(row + u, 1), :] for u in range(2)], axis=1)
        hit = jnp.where(high2 == lax.shift_right_logical(ids, 7), 1.0, 0.0).astype(jnp.bfloat16)
        got = jnp.dot(
            tab_ref[q], jnp.concatenate([hit, hit, hit], axis=0), preferred_element_type=F32
        )
        got = jnp.sum(jnp.where(low2 == (ids & 127), got, 0.0), axis=0, keepdims=True)
        for u in range(2):
            out[pl.ds(at + u, 1), :] = got[:, u * TILE : (u + 1) * TILE]

    here[4].wait()
    here[5].wait()

    def own_rows(i, _):
        for u in range(4):
            t = i * 8 + u * 2
            look_up(3 * tiles + t, 0, f0_ref, t)
            look_up(tiles + t, 1, g0_ref, tiles + t)
        return 0

    near[0].wait_recv()

    @pl.when(has_past)
    def _():
        onward.start()

    lax.fori_loop(0, tiles // 8, own_rows, 0)
    ft_ref[...] = jnp.transpose(
        jnp.concatenate([f0_ref[...], jnp.zeros((TILE - tiles, TILE), F32)], axis=0)
    )

    @pl.when(has_slow)
    def _():
        onward.wait_recv()

    @pl.when(jnp.logical_not(has_slow))
    def _():
        ids_ref[pl.ds(2 * tiles, tiles), :] = jnp.zeros((tiles, TILE), jnp.int32)

    def other_rows(i, _):
        for u in range(4):
            t = i * 8 + u * 2
            look_up(t, 1, g0_ref, t)
            look_up(2 * tiles + t, 1, g0_ref, 2 * tiles + t)
        return 0

    lax.fori_loop(0, tiles // 8, other_rows, 0)
    a0_ref[...] = jnp.exp2(g0_ref[...] * SCALE)
    here[6].wait()
    here[7].wait()
    near[1].wait_recv()
    near[0].wait_send()
    near[1].wait_send()

    @pl.when(has_past)
    def _():
        onward.wait_send()


def walk(
    which, pairs, maxb, tiles, lst, tile_of, x_ref, b0b_ref, k_ref, p1_ref, bufs
):
    def entry(i, u):
        at = which * pairs + i * WIDE + u
        v = lst[lax.shift_right_logical(at, 7), at & (TILE - 1)]
        p = v & (2 * pairs - 1)
        return p, lax.div(p, maxb), lax.div(v, 2 * pairs)

    def scores(i, u, buf):
        p, t, r = entry(i, u)
        buf[u] = lax.dot_general(
            x_ref[jnp.minimum(t, tiles - 1)], tile_of(r), NT, preferred_element_type=F32
        )

    def sums(i, u, buf):
        p, t, r = entry(i, u)
        kv = jnp.exp2(buf[u] * SCALE)
        k_ref[p] = kv
        p1_ref[pl.ds(p, 1), :] = jnp.sum(
            kv * b0b_ref[jnp.minimum(t, tiles - 1)], axis=0, keepdims=True
        )

    one, two = bufs

    def some(j, _):
        for u in range(WIDE):
            scores(2 * j + 1, u, two)
            sums(2 * j, u, one)
        for u in range(WIDE):
            scores(2 * j + 2, u, one)
            sums(2 * j + 1, u, two)
        return 0

    for u in range(WIDE):
        scores(0, u, one)
    lax.fori_loop(0, lax.div(lst[8, which] + 2 * WIDE - 1, 2 * WIDE), some, 0)


def kernel_n(
    tiles, maxb,
    lst, x_ref, of_ref, a0_ref, ft_ref, g0_ref, oh_ref,
    k_ref, p1_ref, f0b_ref, b0b_ref,
    one, two,
):
    pairs = tiles * maxb
    p1_ref[...] = jnp.zeros(p1_ref.shape, F32)
    lanes = lax.broadcasted_iota(jnp.int32, (TILE, TILE), 1)

    def spread(i, _):
        for u in range(4):
            t = i * 4 + u
            col = jnp.sum(jnp.where(lanes == t, ft_ref[...], 0.0), axis=1, keepdims=True)
            f0 = jnp.broadcast_to(col, (TILE, TILE))
            f0b_ref[t] = f0
            b0b_ref[t] = jnp.exp2(f0 * SCALE)
        return 0

    lax.fori_loop(0, tiles // 4, spread, 0)

    def absent(i, _):
        at = 2 * pairs + i
        k_ref[lst[lax.shift_right_logical(at, 7), at & (TILE - 1)] & (2 * pairs - 1)] = jnp.zeros(
            (TILE, TILE), F32
        )
        return 0

    lax.fori_loop(0, lst[8, 2], absent, 0)
    walk(
        0, pairs, maxb, tiles, lst, lambda r: of_ref[jnp.minimum(r, 2 * tiles - 1)],
        x_ref, b0b_ref, k_ref, p1_ref, (one, two),
    )


def fetch(r, ybuf, of_ref, es_ref, tiles):
    @pl.when(r < 2 * tiles)
    def _():
        ybuf[...] = of_ref[jnp.minimum(r, 2 * tiles - 1)]

    @pl.when(r >= 2 * tiles)
    def _():
        ybuf[...] = es_ref[jnp.clip(r - 2 * tiles, 0, tiles - 1)]


def kernel_b(
    tiles, maxb, log_size,
    lst, es_ref, k_in, p1_in, f0b_ref, b0b_ref, g0_ref, a0_ref, x_ref, of_ref, oh_ref,
    k_ref, p1_ref, f1b_ref, b1b_ref, c1_ref, c2_ref, bad_ref,
    ybuf, cols, one, two,
):
    pairs = tiles * maxb
    walk(
        1, pairs, maxb, tiles, lst, lambda r: es_ref[jnp.clip(r - 2 * tiles, 0, tiles - 1)],
        x_ref, b0b_ref, k_ref, p1_ref, (one, two),
    )

    def finish(i, worst):
        for u in range(4):
            t = i * 4 + u
            total = jnp.zeros((TILE, TILE), F32)
            for k in range(maxb):
                at = 3 * pairs + t * maxb + k
                r = jnp.clip(lst[lax.shift_right_logical(at, 7), at & (TILE - 1)], 0, 3 * tiles - 1)
                total = total + k_ref[t * maxb + k] * a0_ref[pl.ds(r, 1), :]
            total = jnp.sum(total, axis=1, keepdims=True)
            worst = jnp.maximum(worst, jnp.where((total >= LO) & (total <= HI), 0.0, 1.0))
            lse = jnp.broadcast_to(jnp.log(total), (TILE, TILE))
            f1 = 0.5 * (f0b_ref[t] + log_size - EPSILON * lse)
            f1b_ref[t] = f1
            b1b_ref[t] = jnp.exp2(f1 * SCALE)
        return worst

    worst = lax.fori_loop(0, tiles // 4, finish, jnp.zeros((TILE, 1), F32))
    onehot = oh_ref[...]
    here = jnp.sum(onehot.astype(F32), axis=1, keepdims=True) > 0.5
    total = add_up(onehot, p1_ref[:pairs])
    fits = (total >= LO) & (total <= HI)
    c1_ref[...] = jnp.where(here, jnp.log(total), NEGATIVE)[: 3 * tiles]
    wrong = jnp.where(here & jnp.logical_not(fits), 1.0, 0.0)
    bad = jnp.maximum(jnp.max(worst), jnp.max(wrong))
    bad_ref[...] = jnp.full((8, TILE), bad)
    c2_ref[...] = jnp.full((3 * tiles, TILE), NEGATIVE, F32)

    @pl.when(bad > 0.5)
    def _():
        for c in range(4):
            cols[c] = jnp.full((3 * tiles, TILE), NEGATIVE if c % 2 == 0 else 0.0, F32)

        def column(c, r, terms):
            top = cols[c, pl.ds(r, 1), :]
            now = jnp.maximum(top, jnp.max(terms, axis=0, keepdims=True))
            cols[c + 1, pl.ds(r, 1), :] = cols[c + 1, pl.ds(r, 1), :] * jnp.exp(top - now) + jnp.sum(
                jnp.exp(terms - now), axis=0, keepdims=True
            )
            cols[c, pl.ds(r, 1), :] = now

        def one(t, _):
            x = x_ref[t]
            f0 = f0b_ref[t]

            def slot(k, carry):
                top, total = carry
                at = 3 * pairs + t * maxb + k
                r = lst[lax.shift_right_logical(at, 7), at & (TILE - 1)]
                fetch(r, ybuf, of_ref, es_ref, tiles)
                s = lax.dot_general(x, ybuf[...], NT, preferred_element_type=F32)
                terms = (g0_ref[pl.ds(r, 1), :] + s) / EPSILON
                now = jnp.maximum(top, jnp.max(terms, axis=1, keepdims=True))
                total = total * jnp.exp(top - now) + jnp.sum(
                    jnp.exp(terms - now), axis=1, keepdims=True
                )
                column(0, r, (f0 + s) / EPSILON)
                return now, total

            count = lst[9, t]
            top, total = lax.fori_loop(
                0, count, slot, (jnp.full((TILE, 1), NEGATIVE, F32), jnp.zeros((TILE, 1), F32))
            )
            lse = jnp.broadcast_to(top + jnp.log(total), (TILE, TILE))
            f1b_ref[t] = 0.5 * (f0 + log_size - EPSILON * lse)

            def again(k, _):
                at = 3 * pairs + t * maxb + k
                r = lst[lax.shift_right_logical(at, 7), at & (TILE - 1)]
                fetch(r, ybuf, of_ref, es_ref, tiles)
                s = lax.dot_general(x, ybuf[...], NT, preferred_element_type=F32)
                column(2, r, (f1b_ref[t] + s) / EPSILON)
                return 0

            lax.fori_loop(0, count, again, 0)
            return 0

        lax.fori_loop(0, tiles, one, 0)
        c1_ref[...] = jnp.where(cols[1] > 0, cols[0] + jnp.log(cols[1]), NEGATIVE)
        c2_ref[...] = jnp.where(cols[3] > 0, cols[2] + jnp.log(cols[3]), NEGATIVE)


def merge(*parts):
    top = functools.reduce(jnp.maximum, parts)
    return top + jnp.log(functools.reduce(jnp.add, [jnp.exp(p - top) for p in parts]))


def kernel_f(
    n, tiles, maxb, log_size,
    lst_ref, k_ref, f1b_ref, b1b_ref, g0_ref, oh_ref, c1_ref, c2s_ref, bad_ref,
    f2_ref, g2_ref, g1_ref,
    lst, p2_ref, c2_ref, a1_ref, ft_ref, got_f, got_s, got_fs, got_sf, got2_f, got2_s,
    send, recv, local,
):
    me, odd, fast, slow, has_slow = partners(n)
    past_fast, past_slow = fast + 1 - 2 * odd, slow - 1 + 2 * odd
    has_past = (past_fast >= 0) & (past_fast < n)
    sems = (send, recv)
    pairs = tiles * maxb
    listing = pltpu.make_async_copy(lst_ref, lst, local)
    listing.start()
    greet(fast)

    @pl.when(has_slow)
    def _():
        greet(slow)
        greet(past_slow)

    @pl.when(has_past)
    def _():
        greet(past_fast)

    to_slow = remote(c1_ref.at[pl.ds(tiles, 2 * tiles)], got_s, sems, 0, slow)
    to_past_fast = remote(c1_ref.at[pl.ds(0, tiles)], got_sf, sems, 1, past_fast)
    to_past_slow = remote(c1_ref.at[pl.ds(2 * tiles, tiles)], got_fs, sems, 2, past_slow)
    to_fast = remote(c1_ref.at[pl.ds(0, 2 * tiles)], got_f, sems, 3, fast)
    pl.semaphore_wait(
        pltpu.get_barrier_semaphore(),
        1 + jnp.where(has_slow, 2, 0) + jnp.where(has_past, 1, 0),
    )

    @pl.when(has_past)
    def _():
        to_past_fast.start()

    @pl.when(has_slow)
    def _():
        to_past_slow.start()
        to_slow.start()

    to_fast.start()

    def columns(i, _):
        for u in range(2):
            t = i * 2 + u
            b1 = b1b_ref[t]
            p2_ref[pl.ds(pl.multiple_of(t * maxb, maxb), maxb), :] = jnp.concatenate(
                [jnp.sum(k_ref[t * maxb + k] * b1, axis=0, keepdims=True) for k in range(maxb)],
                axis=0,
            )
        return 0

    lax.fori_loop(0, tiles // 2, columns, 0)
    total = add_up(oh_ref[...], p2_ref[...])[: 3 * tiles]
    quick = jnp.where(total > 0, jnp.log(total), NEGATIVE)
    c2_ref[...] = jnp.where(bad_ref[0:1, :] > 0.5, c2s_ref[...], quick)

    to_fast.wait_recv()
    @pl.when(has_past)
    def _():
        to_past_slow.wait_recv()

    @pl.when(jnp.logical_not(has_past))
    def _():
        got_fs[...] = jnp.full((tiles, TILE), NEGATIVE, F32)

    @pl.when(has_slow)
    def _():
        to_past_fast.wait_recv()
        to_slow.wait_recv()

    @pl.when(jnp.logical_not(has_slow))
    def _():
        got_sf[...] = jnp.full((tiles, TILE), NEGATIVE, F32)
        got_s[:tiles] = jnp.zeros((tiles, TILE), F32)
        got_s[tiles:] = jnp.full((tiles, TILE), NEGATIVE, F32)
        got2_s[...] = jnp.full((tiles, TILE), NEGATIVE, F32)

    own = pl.ds(tiles, tiles)
    front, back = pl.ds(0, tiles), pl.ds(2 * tiles, tiles)
    for part, lse in (
        (front, merge(c1_ref[front, :], got_f[own, :], got_fs[...])),
        (own, merge(c1_ref[own, :], got_f[front, :], got_s[own, :])),
        (back, merge(c1_ref[back, :], got_s[front, :], got_sf[...])),
    ):
        g1 = 0.5 * (g0_ref[part, :] + log_size - EPSILON * lse)
        g1_ref[part, :] = g1
        a1_ref[part, :] = jnp.exp2(g1 * SCALE)
    last_slow = remote(c2_ref.at[back], got2_s, sems, 4, slow)
    last_fast = remote(c2_ref.at[front], got2_f, sems, 5, fast)

    @pl.when(has_slow)
    def _():
        last_slow.start()

    last_fast.start()
    listing.wait()
    lanes = lax.broadcasted_iota(jnp.int32, (TILE, TILE), 1)
    ft_ref[...] = jnp.zeros((TILE, TILE), F32)

    def rows(i, _):
        for u in range(4):
            t = i * 4 + u
            total = jnp.zeros((TILE, TILE), F32)
            for k in range(maxb):
                at = 3 * pairs + t * maxb + k
                r = jnp.clip(lst[lax.shift_right_logical(at, 7), at & (TILE - 1)], 0, 3 * tiles - 1)
                total = total + k_ref[t * maxb + k] * a1_ref[pl.ds(r, 1), :]
            total = jnp.sum(total, axis=1, keepdims=True)
            fits = (total >= LO) & (total <= HI)
            lse = jnp.broadcast_to(jnp.log(jnp.where(fits, total, jnp.nan)), (TILE, TILE))
            f2 = 0.5 * (f1b_ref[t] + log_size - EPSILON * lse)
            ft_ref[...] = jnp.where(lanes == t, f2, ft_ref[...])
        return 0

    lax.fori_loop(0, tiles // 4, rows, 0)
    f2_ref[...] = jnp.transpose(ft_ref[...])[:tiles]
    last_fast.wait_recv()

    @pl.when(has_slow)
    def _():
        last_slow.wait_recv()

    lse = merge(c2_ref[own, :], got2_f[...], got2_s[...])
    g2_ref[...] = 0.5 * (g1_ref[own, :] + log_size - EPSILON * lse)
    to_fast.wait_send()
    last_fast.wait_send()

    @pl.when(has_slow)
    def _():
        to_slow.wait_send()
        to_past_slow.wait_send()
        last_slow.wait_send()

    @pl.when(has_past)
    def _():
        to_past_fast.wait_send()


def kernel_g(
    tiles, maxb, log_size,
    lst_ref, f2_in, g2_in, g1_ref, bad_ref, f1b_ref, x_ref, of_ref, es_ref,
    f2_ref, g2_ref, lst, ft_ref, ybuf, sem,
):
    pairs = tiles * maxb
    f2 = f2_in[...]
    f2_ref[...] = f2
    g2_ref[...] = g2_in[...]
    bad = jnp.maximum(
        jnp.maximum(jnp.max(jnp.where(f2 == f2, 0.0, 1.0)), jnp.max(bad_ref[...])),
        jnp.max(jnp.where(jnp.abs(g1_ref[...]) <= FAR, 0.0, 1.0)),
    )

    @pl.when(bad > 0.5)
    def _():
        listing = pltpu.make_async_copy(lst_ref, lst, sem)
        listing.start()
        listing.wait()
        lanes = lax.broadcasted_iota(jnp.int32, (TILE, TILE), 1)
        ft_ref[...] = jnp.zeros((TILE, TILE), F32)

        def one(t, _):
            x = x_ref[t]

            def slot(k, carry):
                top, total = carry
                at = 3 * pairs + t * maxb + k
                r = lst[lax.shift_right_logical(at, 7), at & (TILE - 1)]
                fetch(r, ybuf, of_ref, es_ref, tiles)
                s = lax.dot_general(x, ybuf[...], NT, preferred_element_type=F32)
                terms = (g1_ref[pl.ds(r, 1), :] + s) / EPSILON
                now = jnp.maximum(top, jnp.max(terms, axis=1, keepdims=True))
                total = total * jnp.exp(top - now) + jnp.sum(
                    jnp.exp(terms - now), axis=1, keepdims=True
                )
                return now, total

            top, total = lax.fori_loop(
                0, lst[9, t], slot, (jnp.full((TILE, 1), NEGATIVE, F32), jnp.zeros((TILE, 1), F32))
            )
            lse = jnp.broadcast_to(top + jnp.log(total), (TILE, TILE))
            f2 = 0.5 * (f1b_ref[t] + log_size - EPSILON * lse)
            ft_ref[...] = jnp.where(lanes == t, f2, ft_ref[...])
            return 0

        lax.fori_loop(0, tiles, one, 0)
        f2_ref[...] = jnp.transpose(ft_ref[...])[:tiles]


def shards(n, src, tgt, scl, tcl, cs, ct, bl, bc):
    rows, width = src.shape
    tiles = rows // TILE
    maxb = bl.shape[1]
    pairs = tiles * maxb
    log_size = EPSILON * math.log(rows * n)
    bf = jnp.bfloat16
    cost = lambda flops: pl.CostEstimate(flops=flops, bytes_accessed=1 << 23, transcendentals=0)
    flops = 2 * pairs * TILE * TILE * width
    by_tile = lambda a: a.reshape(tiles, TILE, width)
    rows_of = lambda a: a.reshape(tiles, TILE)
    table = lambda a: a.reshape(a.shape[0] // TILE, TILE)
    block, line = (tiles, TILE, TILE), (3 * tiles, TILE)
    dma = pltpu.SemaphoreType.DMA
    route = [(i, i + 1) for i in range(1, n - 1, 2)]
    far = by_tile(lax.ppermute(tgt, "row", route + [(b, a) for a, b in route]))

    ft, g0, a0, x, of, oh, lst = pl.pallas_call(
        functools.partial(kernel_a, n, tiles, maxb),
        out_shape=(
            VM((TILE, TILE), F32),
            VM(line, F32),
            VM(line, F32),
            VM((tiles, TILE, width), bf),
            VM((2 * tiles, TILE, width), bf),
            VM((TILE, pairs), bf),
            VM((16, TILE), jnp.int32),
        ),
        in_specs=[FAR_MEM] * 8,
        out_specs=(SPEC,) * 7,
        scratch_shapes=[
            pltpu.SMEM((maxb, tiles), jnp.int32),
            pltpu.SMEM((tiles,), jnp.int32),
            VM((4 * tiles, TILE), jnp.int32),
            VM((2, tiles, TILE), F32),
            VM((2, TILE, 3 * tiles), bf),
            VM((tiles, TILE), F32),
            VM((pairs, TILE), F32),
            dma((3,)),
            dma((3,)),
            dma((8,)),
        ],
        compiler_params=pltpu.CompilerParams(
            collective_id=0, has_side_effects=True, vmem_limit_bytes=WHOLE
        ),
        cost_estimate=cost(flops),
        name="exchange",
    )(bl.T, bc, by_tile(src), by_tile(tgt), rows_of(scl), rows_of(tcl), table(cs), table(ct))

    steps = [VM((WIDE, TILE, TILE), F32)] * 2
    sums = (
        VM((pairs + 1, TILE, TILE), F32),
        VM((pairs + 8, TILE), F32),
    )
    k, p1, f0b, b0b = pl.pallas_call(
        functools.partial(kernel_n, tiles, maxb),
        out_shape=sums + (VM(block, F32),) * 2,
        in_specs=[SMEM] + [SPEC] * 6,
        out_specs=(SPEC,) * 4,
        scratch_shapes=steps,
        compiler_params=pltpu.CompilerParams(vmem_limit_bytes=LIMIT),
        cost_estimate=cost(flops),
        name="near_pairs",
    )(lst, x, of, a0, ft, g0, oh)

    k, p1, f1b, b1b, c1, c2s, bad = pl.pallas_call(
        functools.partial(kernel_b, tiles, maxb, log_size),
        out_shape=sums
        + (
            VM(block, F32),
            VM(block, F32),
            VM(line, F32),
            VM(line, F32),
            VM((8, TILE), F32),
        ),
        in_specs=[SMEM] + [SPEC] * 10,
        out_specs=(SPEC,) * 7,
        scratch_shapes=[VM((TILE, width), bf), VM((4,) + line, F32)] + steps,
        input_output_aliases={2: 0, 3: 1},
        compiler_params=pltpu.CompilerParams(vmem_limit_bytes=LIMIT),
        cost_estimate=cost(flops),
        name="far_pairs",
    )(lst, far, k, p1, f0b, b0b, g0, a0, x, of, oh)

    f2, g2, g1 = pl.pallas_call(
        functools.partial(kernel_f, n, tiles, maxb, log_size),
        out_shape=(VM((tiles, TILE), F32), VM((tiles, TILE), F32), VM(line, F32)),
        in_specs=[ANY] + [SPEC] * 8,
        out_specs=(SPEC,) * 3,
        scratch_shapes=[
            pltpu.SMEM((16, TILE), jnp.int32),
            VM((pairs, TILE), F32),
            VM(line, F32),
            VM(line, F32),
            VM((TILE, TILE), F32),
            VM((2 * tiles, TILE), F32),
            VM((2 * tiles, TILE), F32),
            VM((tiles, TILE), F32),
            VM((tiles, TILE), F32),
            VM((tiles, TILE), F32),
            VM((tiles, TILE), F32),
            dma((6,)),
            dma((6,)),
            dma,
        ],
        compiler_params=pltpu.CompilerParams(
            collective_id=1, has_side_effects=True, vmem_limit_bytes=LIMIT
        ),
        cost_estimate=cost(flops),
        name="potentials",
    )(lst, k, f1b, b1b, g0, oh, c1, c2s, bad)

    f2, g2 = pl.pallas_call(
        functools.partial(kernel_g, tiles, maxb, log_size),
        out_shape=(jax.ShapeDtypeStruct((tiles, TILE), F32),) * 2,
        in_specs=[ANY] + [SPEC] * 8,
        out_specs=(SPEC,) * 2,
        scratch_shapes=[
            pltpu.SMEM((16, TILE), jnp.int32),
            VM((TILE, TILE), F32),
            VM((TILE, width), bf),
            dma,
        ],
        compiler_params=pltpu.CompilerParams(vmem_limit_bytes=LIMIT),
        cost_estimate=cost(flops),
        name="guard",
    )(lst, f2, g2, g1, bad, f1b, x, of, far)
    return f2.reshape(rows), g2.reshape(rows)


LIMIT = 5 << 20
WHOLE = 48 << 20


def solution(mesh):
    both = P(("grp", "row"))
    wide = P(("grp", "row"), None)
    return jax.shard_map(
        functools.partial(shards, mesh.shape["row"]),
        mesh=mesh,
        in_specs=(wide, wide, both, both, P("grp"), P("grp"), wide, both),
        out_specs=(both, both),
        check_vma=False,
    )
```

time: 314 us -> 292 us (0.930)
  the two profiles are of different devices: /device:TPU:640 before, /device:TPU:575 now
where the time goes in v2:
time: 292 us; the launch traced here: 293 us
  Pallas kernels  280 us (96%)
  waiting for transfers between devices  7.15 us (2%)
  starting transfers between devices  4.99 us (2%)
    pallas_call x1, Pallas kernels, shards(): pl.pallas_call(functools.partial(kernel_b, tiles, maxb, log_size), out_sh...  156 us
    pallas_call x1, Pallas kernels, shards(): pl.pallas_call(functools.partial(kernel_g, tiles, maxb, log_size), out_sh...  93.1 us
    pallas_call x1, Pallas kernels, shards(): pl.pallas_call(functools.partial(kernel_f, n, tiles, maxb, log_size), out...  11.8 us
    pallas_call x1, Pallas kernels, shards(): pl.pallas_call(functools.partial(kernel_a, n, tiles, maxb), out_shape=(VM...  10.7 us
    pallas_call x1, Pallas kernels, shards(): pl.pallas_call(functools.partial(kernel_n, tiles, maxb), out_shape=sums +...  8.17 us
    ppermute x1, waiting for transfers between devices, shards(): far = by_tile(lax.ppermute(tgt, 'row', route + [(b, a) for a, b in route]))  7.15 us
  transfers between devices with their start and end apart: 1, of which 1 were waited for; matrix products, arithmetic and copies ran while one was open for 0% of the time, Pallas kernels for 6%

profile of v2, /device:TPU:575, one launch (start us, length us, event | category | flops | bytes accessed | tf_op | source)
XLA Modules:
  0.0 292.8 jit_solution(16502216996539940251)
XLA Ops:
  0.6 5.0 %collective-permute-start = (bf16[4096,256]{1,0:T(8,128)(2,1)}, bf16[4096,256]{1,0:T(8,128)(2,1)S(1)}, u32[]{:S(2)}, u32[]{:S(2)}) collective-permute-start(bf16[4096,256]{1,0:T(8,128)(2,1)} %param.9), channel_id=1, source_target_pairs={{1,2},{3,4},{5,6},{7,8},{9,10},{11,12},{13,14},{15,16},{17,18},{19... | collective-permute-start | bytes 6291464 | tf_op jit(solution)/shard_map/ppermute | solution.py:615
  5.6 10.7 %exchange.1 = (f32[128,128]{1,0:T(8,128)S(1)}, f32[96,128]{1,0:T(8,128)S(1)}, f32[96,128]{1,0:T(8,128)S(1)}, bf16[32,128,256]{2,1,0:T(8,128)(2,1)S(1)}, bf16[64,...) custom-call(s32[8,32]{1,0:T(8,128)} %bitcast.20, s32[32]{0:T(128)} %bc_hbm.1, ...), custom_call_target="tpu_custom_call" | custom-call | flops 2147483648 | bytes 8388608 | tf_op jit(solution)/shard_map/exchange/pallas_call | solution.py:617
  16.4 8.2 %near_pairs.1 = (f32[257,128,128]{2,1,0:T(8,128)S(1)}, f32[264,128]{1,0:T(8,128)S(1)}, f32[32,128,128]{2,1,0:T(8,128)S(1)}, f32[32,128,128]{2,1,0:T(8,128)S(1)}) custom-call(s32[16,128]{1,0:T(8,128)S(1)} %get-tuple-element.24.lst.lst_ref, bf16[32,128,256]{2,1,0:T(8,128)(2,1)S(1)} %get-tuple-element.25.x_ref, ...), custom_call_target="tpu_custom_call" | custom-call | flops 2147483648 | bytes 8388608 | tf_op jit(solution)/shard_map/near_pairs/pallas_call | solution.py:654
  24.6 7.2 %collective-permute-done = bf16[4096,256]{1,0:T(8,128)(2,1)S(1)} collective-permute-done((bf16[4096,256]{1,0:T(8,128)(2,1)}, bf16[4096,256]{1,0:T(8,128)(2,1)S(1)}, u32[]{:S(2)}, u32[]{:S(2)}) %collective-permute-start) | collective-permute-done | bytes 2097184 | tf_op jit(solution)/shard_map/ppermute | solution.py:615
  31.7 156.1 %far_pairs.1 = (f32[257,128,128]{2,1,0:T(8,128)S(1)}, f32[264,128]{1,0:T(8,128)S(1)}, f32[32,128,128]{2,1,0:T(8,128)S(1)}, f32[32,128,128]{2,1,0:T(8,128)S(1)}, ...) custom-call(s32[16,128]{1,0:T(8,128)S(1)} %get-tuple-element.24.lst., ...), custom_call_target="tpu_custom_call", output_to_operand_aliasing={{0}: (2, {}), {1}: (3, {})} | custom-call | flops 2147483648 | bytes 8388608 | tf_op jit(solution)/shard_map/far_pairs/pallas_call | solution.py:665
  187.8 11.8 %potentials.1 = (f32[32,128]{1,0:T(8,128)S(1)}, f32[32,128]{1,0:T(8,128)S(1)}, f32[96,128]{1,0:T(8,128)S(1)}) custom-call(s32[16,128]{1,0:T(8,128)S(1)} %get-tuple-element.24.lst.lst_ref, f32[257,128,128]{2,1,0:T(8,128)S(1)} %get-tuple-element.35.k_ref, f32[32,128,128]{2,1,0:T(8,128)S(1)} %get-tuple-element.36.f1b_ref, ...), custom_call_target="tpu_custom_call" | custom-call | flops 2147483648 | bytes 8388608 | tf_op jit(solution)/shard_map/potentials/pallas_call | solution.py:684
  199.7 93.1 %guard.1 = (f32[32,128]{1,0:T(8,128)}, f32[32,128]{1,0:T(8,128)}) custom-call(s32[16,128]{1,0:T(8,128)S(1)} %get-tuple-element.24.lst.lst_ref, f32[32,128]{1,0:T(8,128)S(1)} %get-tuple-element.41.f2_in, f32[32,128]{1,0:T(8,128)S(1)} %get-tuple-element.42.g2_in, f32[96,128]{1,0:T(8,128)S(1)} %get-tuple-element.43.g1_ref, ...), custom_call_target="tpu_custom_call" | custom-call | flops 2147483648 | bytes 8388608 | tf_op jit(solution)/shard_map/guard/pallas_call | solution.py:712
Async XLA Ops:
  0.6 31.1 %collective-permute-start = (bf16[4096,256]{1,0:T(8,128)(2,1)}, bf16[4096,256]{1,0:T(8,128)(2,1)S(1)}, u32[]{:S(2)}, u32[]{:S(2)}) collective-permute-start(bf16[4096,256]{1,0:T(8,128)(2,1)} %param.9), channel_id=1, source_target_pairs={{1,2},{3,4},{5,6},{7,8},{9,10},{11,12},{13,14},{15,16},{17,18},{19... | collective-permute-start | bytes 6291464 | tf_op jit(solution)/shard_map/ppermute | solution.py:615
